TPU v7x, 8 devices: a whole 2x2x1 slice. The times are simulated.
8 devices in a mesh: data: 2 (over z, y), dap: 4 (over x, core).
Axes of the slice: x: 2, y: 2, z: 1, core: 2. Of those that a mesh axis runs over, the one named last changes fastest.
Arguments:
- msa_act: bfloat16 [32, 128, 64], P(('data', 'dap')), parts along dimension 0
- pair_act: bfloat16 [256, 128, 128], P(('data', 'dap')), parts along dimension 0
- msa_mask: int32 [32, 128], P('data'), parts along dimension 0
- res_mask: int32 [256], P('data'), parts along dimension 0
- w_row_bias: bfloat16 [2, 128, 8], replicated
- w_row_in: bfloat16 [2, 64, 4, 8, 8], replicated
- w_row_out: bfloat16 [2, 8, 8, 64], replicated
- w_col_in: bfloat16 [2, 64, 4, 8, 8], replicated
- w_col_out: bfloat16 [2, 8, 8, 64], replicated
- w_opm_in: bfloat16 [2, 64, 2, 32], replicated
- w_opm_out: bfloat16 [2, 32, 32, 128], replicated
- w_ts_bias: bfloat16 [2, 128, 4], replicated
- w_ts_in: bfloat16 [2, 128, 4, 4, 32], replicated
- w_ts_out: bfloat16 [2, 4, 32, 128], replicated
- w_te_bias: bfloat16 [2, 128, 4], replicated
- w_te_in: bfloat16 [2, 128, 4, 4, 32], replicated
- w_te_out: bfloat16 [2, 4, 32, 128], replicated
Outputs:
- output 1: bfloat16 [32, 128, 64], P(('data', 'dap')), parts along dimension 0
- output 2: bfloat16 [256, 128, 128], P(('data', 'dap')), parts along dimension 0
There are 2 independent parts. A program takes and returns all parts, laid end to end along the dimension named above; an argument that names none is the same for every part.
All inputs are finite; a program needn't handle non-finite values.
Results may differ from a plain program's by a relative error of at most 0.01828.
Values are sent between devices in bfloat16 or wider.
A program may use at most 1 GiB of HBM per device.

v0:
```python
import jax
import jax.numpy as jnp
from jax import lax
from jax.sharding import PartitionSpec as P


def layer_norm(values):
    flat = values.astype(jnp.float32)
    row_mean = jnp.mean(flat, axis=-1, keepdims=True)
    centered = flat - row_mean
    row_var = jnp.mean(centered * centered, axis=-1, keepdims=True)
    return (centered * lax.rsqrt(row_var + 1e-5)).astype(jnp.bfloat16)


def add_residual(current, update):
    return (current.astype(jnp.float32) + update).astype(jnp.bfloat16)


def pair_bias(pair_ln, w_bias, form):
    return jnp.einsum(form, pair_ln, w_bias, preferred_element_type=jnp.float32).astype(jnp.bfloat16)


def gated_attention(x_ln, w_in, w_out, bias_hqk, key_mask, batch_first):
    head_dim = w_in.shape[3]
    projected = jnp.einsum('abc,cfhd->abfhd', x_ln, w_in, preferred_element_type=jnp.float32).astype(jnp.bfloat16)
    query = projected[:, :, 0]
    keys = projected[:, :, 1]
    values = projected[:, :, 2]
    gate_raw = projected[:, :, 3]
    if batch_first:
        logits = jnp.einsum('bqhd,bkhd->bhqk', query, keys, preferred_element_type=jnp.float32)
    else:
        logits = jnp.einsum('qbhd,kbhd->bhqk', query, keys, preferred_element_type=jnp.float32)
    logits = logits * head_dim ** -0.5
    if bias_hqk is not None:
        logits = logits + bias_hqk.astype(jnp.float32)
    logits = jnp.where(key_mask > 0, logits, -1e9)
    attn_probs = jax.nn.softmax(logits, axis=-1).astype(jnp.bfloat16)
    if batch_first:
        attended = jnp.einsum('bhqk,bkhd->bqhd', attn_probs, values, preferred_element_type=jnp.float32)
    else:
        attended = jnp.einsum('bhqk,kbhd->qbhd', attn_probs, values, preferred_element_type=jnp.float32)
    gated = (attended * jax.nn.sigmoid(gate_raw.astype(jnp.float32))).astype(jnp.bfloat16)
    return jnp.einsum('abhd,hdc->abc', gated, w_out, preferred_element_type=jnp.float32)


def opm_halves(value_a8, mask_cols, w_in):
    projected = jnp.einsum('sic,cfp->sifp', layer_norm(value_a8), w_in, preferred_element_type=jnp.float32)
    projected = (projected * mask_cols.astype(jnp.float32)[:, :, None, None]).astype(jnp.bfloat16)
    return projected[:, :, 0], projected[:, :, 1]


def opm_update(pair_act, left, right, left_mask, right_mask, w_out):
    outer = jnp.einsum('sip,sjq->ijpq', left, right, preferred_element_type=jnp.float32).astype(jnp.bfloat16)
    update = jnp.einsum('ijpq,pqc->ijc', outer, w_out, preferred_element_type=jnp.float32)
    pair_norm = jnp.einsum('si,sj->ij', left_mask.astype(jnp.bfloat16), right_mask.astype(jnp.bfloat16), preferred_element_type=jnp.float32)
    return add_residual(pair_act, update / (1e-3 + pair_norm)[:, :, None])


def solution(mesh):
    def local_step(value_a7, pair_blk, array_b8, res_mask, w_row_bias, w_row_in, w_row_out, w_col_in, w_col_out, w_opm_in, w_opm_out, w_ts_bias, w_ts_in, w_ts_out, w_te_bias, w_te_in, w_te_out):
        dev_index = lax.axis_index('dap')
        seq_loc = value_a7.shape[0]
        res_loc = pair_blk.shape[0]
        mask_seq = lax.dynamic_slice_in_dim(array_b8, dev_index * seq_loc, seq_loc, 0)
        mask_cols = lax.dynamic_slice_in_dim(array_b8, dev_index * res_loc, res_loc, 1)
        row_keys = mask_seq[:, None, None, :]
        col_keys = mask_cols.T[:, None, None, :]
        tri_keys = res_mask[None, None, None, :]

        row_bias = lax.all_gather(pair_bias(layer_norm(pair_blk), w_row_bias[0], 'ijc,ch->hij'), 'dap', axis=1, tiled=True)
        value_a7 = add_residual(value_a7, gated_attention(layer_norm(value_a7), w_row_in[0], w_row_out[0], row_bias, row_keys, True))
        value_a7 = lax.all_to_all(value_a7, 'dap', 1, 0, tiled=True)
        value_a7 = add_residual(value_a7, gated_attention(layer_norm(value_a7), w_col_in[0], w_col_out[0], None, col_keys, False))
        left, right = opm_halves(value_a7, mask_cols, w_opm_in[0])
        right_full = lax.all_gather(right, 'dap', axis=1, tiled=True)
        pair_blk = opm_update(pair_blk, left, right_full, mask_cols, array_b8, w_opm_out[0])
        pair_ln = layer_norm(pair_blk)
        tri_bias = lax.all_gather(pair_bias(pair_ln, w_ts_bias[0], 'ijc,ch->hij'), 'dap', axis=1, tiled=True)
        pair_blk = add_residual(pair_blk, gated_attention(pair_ln, w_ts_in[0], w_ts_out[0], tri_bias, tri_keys, True))
        pair_blk = lax.all_to_all(pair_blk, 'dap', 1, 0, tiled=True)
        pair_ln = layer_norm(pair_blk)
        tri_bias = lax.all_gather(pair_bias(pair_ln, w_te_bias[0], 'kic,ch->hik'), 'dap', axis=1, tiled=True)
        pair_blk = add_residual(pair_blk, gated_attention(pair_ln, w_te_in[0], w_te_out[0], tri_bias, tri_keys, False))

        row_bias = lax.all_gather(pair_bias(layer_norm(pair_blk), w_row_bias[1], 'ijc,ch->hij'), 'dap', axis=2, tiled=True)
        value_a7 = add_residual(value_a7, gated_attention(layer_norm(value_a7), w_col_in[1], w_col_out[1], None, col_keys, False))
        left, right = opm_halves(value_a7, mask_cols, w_opm_in[1])
        left_full = lax.all_gather(left, 'dap', axis=1, tiled=True)
        pair_blk = opm_update(pair_blk, left_full, right, array_b8, mask_cols, w_opm_out[1])
        value_a7 = lax.all_to_all(value_a7, 'dap', 0, 1, tiled=True)
        value_a7 = add_residual(value_a7, gated_attention(layer_norm(value_a7), w_row_in[1], w_row_out[1], row_bias, row_keys, True))
        pair_ln = layer_norm(pair_blk)
        tri_bias = lax.all_gather(pair_bias(pair_ln, w_te_bias[1], 'kic,ch->hik'), 'dap', axis=1, tiled=True)
        pair_blk = add_residual(pair_blk, gated_attention(pair_ln, w_te_in[1], w_te_out[1], tri_bias, tri_keys, False))
        pair_blk = lax.all_to_all(pair_blk, 'dap', 0, 1, tiled=True)
        pair_ln = layer_norm(pair_blk)
        tri_bias = lax.all_gather(pair_bias(pair_ln, w_ts_bias[1], 'ijc,ch->hij'), 'dap', axis=1, tiled=True)
        pair_blk = add_residual(pair_blk, gated_attention(pair_ln, w_ts_in[1], w_ts_out[1], tri_bias, tri_keys, True))
        return value_a7, pair_blk

    in_specs = (P(('data', 'dap')), P(('data', 'dap')), P('data'), P('data')) + (P(),) * 13
    out_specs = (P(('data', 'dap')), P(('data', 'dap')))
    return jax.shard_map(local_step, mesh=mesh, in_specs=in_specs, out_specs=out_specs, check_vma=False)
```

profile of v0, /device:TPU:0, one launch (start us, length us, event | category | flops | bytes accessed | tf_op | source)
XLA Modules:
  0.0 285.0 jit_solution(2457514235723629798)
XLA Ops:
  3.2 10.8 %all_gather.24 = bf16[8,128,128]{2,0,1:T(8,128)(2,1)S(1)} all-gather(bf16[8,32,128]{2,0,1:T(8,128)(2,1)S(1)} %fusion.94), channel_id=1, replica_groups=mesh['data'=2,'dap'=4] {'dap'}, dimensions={1}, use_global_device_ids=true | all-gather | bytes 327680 | tf_op jit(solution)/shard_map/all_gather | solution.py:71
  20.1 3.7 %all-to-all-start = ((bf16[4,2,4096]{2,1,0:T(2,128)(2,1)}), bf16[4,2,4096]{2,1,0:T(2,128)(2,1)S(1)}, u32[]{:S(2)}, u32[]{:S(2)}) async-start(bf16[4,2,4096]{2,1,0:T(2,128)(2,1)} %reshape.373), calls=%async_computation | async-start | bytes 131072 | tf_op jit(solution)/shard_map/all_to_all | solution.py:73
  32.9 4.5 %fusion.278 = (f32[32,8,16]{2,1,0:T(8,128)}, f32[32,8,16,16]{2,3,1,0:T(8,128)}) fusion(pred[32,16]{1,0:T(8,128)(4,1)S(1)} %copy.271, bf16[16,32,8,8]{0,3,2,1:T(8,128)(2,1)} %copy.272, bf16[16,32,8,8]{0,3,2,1:T(8,128)(2,1)S(1)} %copy.273), kind=kOutput, calls=%fused_computation.400 | convolution fusion | flops 1310735 | bytes 410112 | tf_op jit(solution)/shard_map/sub | solution.py:38
  47.6 4.5 %fusion.280 = (f32[32,8,16]{2,1,0:T(8,128)}, f32[32,8,16,16]{2,3,1,0:T(8,128)}) fusion(pred[32,16]{1,0:T(8,128)(4,1)S(1)} %copy-done.19, bf16[16,32,8,8]{0,3,2,1:T(8,128)(2,1)} %copy.277, bf16[16,32,8,8]{0,3,2,1:T(8,128)(2,1)S(1)} %copy.278), kind=kOutput, calls=%fused_computation.402 | convolution fusion | flops 1310735 | bytes 410112 | tf_op jit(solution)/shard_map/sub | solution.py:38
  59.2 9.3 %all-gather = bf16[16,128,1,32]{3,1,2,0:T(8,128)(2,1)S(1)} all-gather(bf16[16,32,1,32]{3,1,2,0:T(8,128)(2,1)S(1)} %get-tuple-element.13), channel_id=2, replica_groups=mesh['data'=2,'dap'=4] {'dap'}, dimensions={1}, use_global_device_ids=true | all-gather | bytes 163840 | tf_op jit(solution)/shard_map/all_gather | solution.py:76
  68.8 3.8 %convert_reduce_fusion.2 = (f32[32,128]{1,0:T(8,128)S(1)}, bf16[32,128,128]{1,2,0:T(8,128)(2,1)S(1)}) fusion(f32[32,128]{1,0:T(8,128)S(1)} %copy-done.14, bf16[1,32,32,128]{3,2,1,0:T(8,128)(2,1)S(1)} %slice-done, bf16[16,128,32,1]{1,0,3,2:T(8,128)(2,1)S(1)} %copy.337, bf16[16,32,32]{2,1,0:T(8,128)(2,1)S(1)} %get-tuple-element.12, ...), kind=kOutput, calls=%fused_computation.60 | convolution fusion | flops 1215295488 | bytes 2555904 | tf_op jit(solution)/shard_map/ijpq,pqc->ijc/dot_general | solution.py:55
  73.4 8.2 %all_gather.26 = bf16[4,128,128]{2,0,1:T(4,128)(2,1)S(1)} all-gather(bf16[4,32,128]{2,0,1:T(4,128)(2,1)S(1)} %fusion.96), channel_id=1, replica_groups=mesh['data'=2,'dap'=4] {'dap'}, dimensions={1}, use_global_device_ids=true | all-gather | bytes 163840 | tf_op jit(solution)/shard_map/all_gather | solution.py:79
  84.9 4.5 %fusion.108 = f32[32,4,128,128]{2,3,1,0:T(8,128)} fusion(bf16[32,128,4,4,32]{1,4,3,2,0:T(8,128)(2,1)S(1)} %convolution_convert_fusion.3), kind=kOutput, calls=%fused_computation.183 | convolution fusion | flops 134217728 | bytes 10485760 | tf_op jit(solution)/shard_map/bqhd,bkhd->bhqk/dot_general | solution.py:31
  89.4 3.5 %all-to-all-start.1 = ((bf16[4,2,4096]{2,1,0:T(2,128)(2,1)}), bf16[4,2,4096]{2,1,0:T(2,128)(2,1)S(1)}, u32[]{:S(2)}, u32[]{:S(2)}) async-start(bf16[4,2,4096]{2,1,0:T(2,128)(2,1)} %reshape.375), calls=%async_computation.1 | async-start | bytes 131072 | tf_op jit(solution)/shard_map/all_to_all | solution.py:91
  93.0 12.5 %fusion.283 = (f32[32,4,128]{2,1,0:T(4,128)S(1)}, f32[32,4,128,128]{2,3,1,0:T(8,128)}) fusion(f32[32,4,128,128]{2,3,1,0:T(8,128)} %fusion.108, f32[4,128,128]{1,2,0:T(8,128)S(1)} %copy.294, pred[128]{0:T(512)(128)(4,1)S(1)} %copy-done.34), kind=kOutput, calls=%fused_computation.403 | output fusion | flops 16777344 | bytes 17105024 | tf_op jit(solution)/shard_map/sub | solution.py:38
  105.5 5.5 %fusion.59 = bf16[32,128,128]{1,2,0:T(8,128)(2,1)S(1)} fusion(bf16[32,128,128]{1,2,0:T(8,128)(2,1)S(1)} %get-tuple-element.25, f32[32,4,128,128]{2,3,1,0:T(8,128)} %get-tuple-element.27, f32[32,4,128]{2,1,0:T(4,128)S(1)} %get-tuple-element.26, bf16[32,128,4,4,32]{1,4,3,2,0:T(8,128)(2,1)} %copy-done.2, bf16[2,4,32,128]{3,2,1,0:T(8,128)(2,1)S(1)} %copy-done.26), kind=kOutput, calls=%fused_computation.85 | convolution fusion | flops 277348352 | bytes 12681216 | tf_op jit(solution)/shard_map/abhd,hdc->abc/dot_general | solution.py:44
  111.7 10.5 %all-gather.1 = bf16[16,128,1,32]{3,1,2,0:T(8,128)(2,1)S(1)} all-gather(bf16[16,32,1,32]{3,1,2,0:T(8,128)(2,1)S(1)} %get-tuple-element.11), channel_id=3, replica_groups=mesh['data'=2,'dap'=4] {'dap'}, dimensions={1}, use_global_device_ids=true | all-gather | bytes 163840 | tf_op jit(solution)/shard_map/all_gather | solution.py:89
  124.7 3.9 %all-to-all-start.2 = ((bf16[32,128,128]{2,0,1:T(8,128)(2,1)}), bf16[32,128,128]{2,0,1:T(8,128)(2,1)S(1)}, u32[]{:S(2)}, u32[]{:S(2)}) async-start(bf16[32,128,128]{2,0,1:T(8,128)(2,1)} %copy.297), calls=%async_computation.2 | async-start | bytes 2097152 | tf_op jit(solution)/shard_map/all_to_all | solution.py:81
  129.9 12.9 %all-to-all-done.2 = bf16[32,128,128]{2,0,1:T(8,128)(2,1)S(1)} async-done(((bf16[32,128,128]{2,0,1:T(8,128)(2,1)}), bf16[32,128,128]{2,0,1:T(8,128)(2,1)S(1)}, u32[]{:S(2)}, u32[]{:S(2)}) %all-to-all-start.2) | async-done | bytes 1048608 | tf_op jit(solution)/shard_map/all_to_all | solution.py:81
  148.3 4.5 %fusion.106 = f32[32,4,128,128]{2,3,1,0:T(8,128)} fusion(bf16[128,32,4,4,32]{0,4,3,2,1:T(8,128)(2,1)S(1)} %convolution_convert_fusion.2), kind=kOutput, calls=%fused_computation.178 | convolution fusion | flops 134217728 | bytes 10485760 | tf_op jit(solution)/shard_map/qbhd,kbhd->bhqk/dot_general | solution.py:33
  154.4 7.3 %all_gather.27 = bf16[4,128,128]{2,0,1:T(4,128)(2,1)S(1)} all-gather(bf16[4,32,128]{2,0,1:T(4,128)(2,1)S(1)} %copy.302), channel_id=1, replica_groups=mesh['data'=2,'dap'=4] {'dap'}, dimensions={1}, use_global_device_ids=true | all-gather | bytes 163840 | tf_op jit(solution)/shard_map/all_gather | solution.py:83
  164.2 2.5 copy.306
  166.7 13.1 %fusion.284 = (f32[32,4,128]{2,1,0:T(4,128)}, f32[32,4,128,128]{2,3,1,0:T(8,128)}) fusion(f32[32,4,128,128]{2,3,1,0:T(8,128)} %fusion.106, f32[4,128,128]{1,2,0:T(8,128)S(1)} %copy-done.4, pred[128]{0:T(512)(128)(4,1)S(1)} %copy-done.34), kind=kOutput, calls=%fused_computation.404 | output fusion | flops 16777344 | bytes 17105024 | tf_op jit(solution)/shard_map/sub | solution.py:38
  179.9 6.1 %convert_reduce_fusion.1 = (f32[128,32]{0,1:T(8,128)}, bf16[128,32,128]{0,2,1:T(8,128)(2,1)S(1)}) fusion(f32[128,32,128]{0,2,1:T(8,128)S(1)} %copy.306, bf16[2,4,32,128]{3,2,1,0:T(8,128)(2,1)} %param.33, f32[32,4,128,128]{2,3,1,0:T(8,128)} %get-tuple-element.29, f32[32,4,128]{2,1,0:T(4,128)} %get-tuple-element.28, bf16[128,32,4,4,32]{0,4,3,2,1:T(8,128)(2,1)} %copy-done), kind=kOutput, calls=%fused_computation.57 | convolution fusion | flops 277868544 | bytes 13746176 | tf_op jit(solution)/shard_map/abhd,hdc->abc/dot_general | solution.py:44
  186.0 4.8 %convert_reduce_fusion = (f32[128,32]{0,1:T(8,128)S(1)}, bf16[128,32,128]{0,2,1:T(8,128)(2,1)S(1)}) fusion(f32[128,32]{0,1:T(8,128)S(1)} %bitcast.544, bf16[2,32,32,128]{3,2,1,0:T(8,128)(2,1)} %param.27, bf16[16,128,32]{1,0,2:T(8,128)(2,1)} %copy.312, bf16[16,32,32,1]{2,1,0,3:T(8,128)(2,1)} %get-tuple-element.10, ...), kind=kOutput, calls=%fused_computation.54 | convolution fusion | flops 1215295488 | bytes 2654208 | tf_op jit(solution)/shard_map/ijpq,pqc->ijc/dot_general | solution.py:55
  191.8 3.2 %convolution_convert_fusion.1 = bf16[128,32,4,4,32]{0,4,3,2,1:T(8,128)(2,1)} fusion(bf16[128,32,128]{0,2,1:T(8,128)(2,1)S(1)} %get-tuple-element.37, f32[128,32]{0,1:T(8,128)S(1)} %add_rsqrt_fusion.2, f32[128,32]{0,1:T(8,128)S(1)} %broadcast_multiply_fusion.2, bf16[2,128,4,4,32]{1,4,3,2,0:T(8,128)(2,1)S(1)} %copy-done.6), kind=kOutput, calls=%fused_computation.65 | convolution fusion | flops 541065216 | bytes 5406720 | tf_op jit(solution)/shard_map/abc,cfhd->abfhd/dot_general | solution.py:25
  195.0 8.7 %all_gather.30 = bf16[4,128,128]{2,0,1:T(4,128)(2,1)S(1)} all-gather(bf16[4,32,128]{2,0,1:T(4,128)(2,1)S(1)} %fusion.97), channel_id=1, replica_groups=mesh['data'=2,'dap'=4] {'dap'}, dimensions={1}, use_global_device_ids=true | all-gather | bytes 163840 | tf_op jit(solution)/shard_map/all_gather | solution.py:94
  203.9 2.9 %fusion.104 = f32[32,4,128,128]{2,3,1,0:T(8,128)S(1)} fusion(bf16[128,32,4,4,32]{0,4,3,2,1:T(8,128)(2,1)} %convolution_convert_fusion.1), kind=kOutput, calls=%fused_computation.173 | convolution fusion | flops 134217728 | bytes 10485760 | tf_op jit(solution)/shard_map/qbhd,kbhd->bhqk/dot_general | solution.py:33
  206.8 6.3 %fusion.290 = (f32[32,4,128]{2,1,0:T(4,128)}, f32[32,4,128,128]{2,3,1,0:T(8,128)}) fusion(f32[32,4,128,128]{2,3,1,0:T(8,128)S(1)} %fusion.104, f32[4,128,128]{1,2,0:T(8,128)S(1)} %copy.316, pred[128]{0:T(512)(128)(4,1)S(1)} %copy-done.35), kind=kOutput, calls=%fused_computation.406 | output fusion | flops 16777344 | bytes 17105024 | tf_op jit(solution)/shard_map/sub | solution.py:38
  213.1 5.5 %fusion.61 = bf16[128,32,128]{0,2,1:T(8,128)(2,1)S(1)} fusion(bf16[128,32,128]{0,2,1:T(8,128)(2,1)S(1)} %get-tuple-element.37, f32[32,4,128,128]{2,3,1,0:T(8,128)} %get-tuple-element.39, f32[32,4,128]{2,1,0:T(4,128)} %get-tuple-element.38, bf16[128,32,4,4,32]{0,4,3,2,1:T(8,128)(2,1)} %convolution_convert_fusion.1, bf16[2,4,32,128]{3,2,1,0:T(8,128)(2,1)} %param.33), kind=kOutput, calls=%fused_computation.87 | convolution fusion | flops 277348352 | bytes 12681216 | tf_op jit(solution)/shard_map/abhd,hdc->abc/dot_general | solution.py:44
  220.3 3.6 %all-to-all-start.3 = ((bf16[128,32,128]{2,1,0:T(8,128)(2,1)}), bf16[128,32,128]{2,1,0:T(8,128)(2,1)S(1)}, u32[]{:S(2)}, u32[]{:S(2)}) async-start(bf16[128,32,128]{2,1,0:T(8,128)(2,1)} %copy.319), calls=%async_computation.3 | async-start | bytes 2097152 | tf_op jit(solution)/shard_map/all_to_all | solution.py:96
  224.7 16.8 %all_gather.28 = bf16[8,128,128]{1,0,2:T(8,128)(2,1)S(1)} all-gather(bf16[8,128,32]{1,0,2:T(8,128)(2,1)S(1)} %fusion.95), channel_id=1, replica_groups=mesh['data'=2,'dap'=4] {'dap'}, dimensions={2}, use_global_device_ids=true | all-gather | bytes 327680 | tf_op jit(solution)/shard_map/all_gather | solution.py:86
  243.9 2.7 fusion.93
  251.3 4.5 %fusion.102 = f32[32,4,128,128]{2,3,1,0:T(8,128)} fusion(bf16[32,128,4,4,32]{1,4,3,2,0:T(8,128)(2,1)S(1)} %convolution_convert_fusion), kind=kOutput, calls=%fused_computation.168 | convolution fusion | flops 134217728 | bytes 10485760 | tf_op jit(solution)/shard_map/bqhd,bkhd->bhqk/dot_general | solution.py:31
  256.2 8.6 %all_gather.31 = bf16[4,128,128]{2,0,1:T(4,128)(2,1)S(1)} all-gather(bf16[4,32,128]{2,0,1:T(4,128)(2,1)S(1)} %fusion.98), channel_id=1, replica_groups=mesh['data'=2,'dap'=4] {'dap'}, dimensions={1}, use_global_device_ids=true | all-gather | bytes 163840 | tf_op jit(solution)/shard_map/all_gather | solution.py:98
  265.8 12.5 %fusion.291 = (f32[32,4,128]{2,1,0:T(4,128)S(1)}, f32[32,4,128,128]{2,3,1,0:T(8,128)}) fusion(f32[32,4,128,128]{2,3,1,0:T(8,128)} %fusion.102, f32[4,128,128]{1,2,0:T(8,128)S(1)} %copy.323, pred[128]{0:T(512)(128)(4,1)S(1)} %copy-done.36), kind=kOutput, calls=%fused_computation.407 | output fusion | flops 16777344 | bytes 17105024 | tf_op jit(solution)/shard_map/sub | solution.py:38
  278.4 6.4 %fusion.62 = bf16[32,128,128]{2,1,0:T(8,128)(2,1)} fusion(f32[32,4,32,128]{3,2,1,0:T(8,128)S(1)} %copy.320, f32[32,4,128,128]{2,3,1,0:T(8,128)} %get-tuple-element.41, f32[32,4,128]{2,1,0:T(4,128)S(1)} %get-tuple-element.40, bf16[32,128,4,4,32]{1,4,3,2,0:T(8,128)(2,1)} %copy-done.1, bf16[2,4,32,128]{3,2,1,0:T(8,128)(2,1)S(1)} %copy-done.27), kind=kOutput, calls=%fused_computation.89 | convolution fusion | flops 276824064 | bytes 13729792 | tf_op jit(solution)/shard_map/abhd,hdc->abc/dot_general | solution.py:44
  (197 shorter events, 64.6 us)
Async XLA Ops:
  2.5 11.8 %copy-start.3 = (bf16[4,128,64]{1,2,0:T(8,128)(2,1)S(1)}, bf16[4,128,64]{1,2,0:T(8,128)(2,1)}, u32[]{:S(2)}) copy-start(bf16[4,128,64]{1,2,0:T(8,128)(2,1)} %param.17) | copy-start | bytes 196612
  2.5 11.9 %copy-start.12 = (s32[16,128]{1,0:T(8,128)S(1)}, s32[16,128]{1,0:T(8,128)}, u32[]{:S(2)}) copy-start(s32[16,128]{1,0:T(8,128)} %param.19) | copy-start | bytes 24580
  2.5 11.9 %copy-start.10 = (bf16[2,64,4,8,8]{1,4,3,2,0:T(8,128)(2,1)S(1)}, bf16[2,64,4,8,8]{1,4,3,2,0:T(8,128)(2,1)}, u32[]{:S(2)}) copy-start(bf16[2,64,4,8,8]{1,4,3,2,0:T(8,128)(2,1)} %param.22) | copy-start | bytes 196612
  17.0 8.4 %copy-start.33 = (s32[128]{0:T(128)S(1)}, s32[128]{0:T(128)}, u32[]{:S(2)}) copy-start(s32[128]{0:T(128)} %param.20) | copy-start | bytes 1540
  19.1 9.0 %copy-start.9 = (bf16[2,64,4,8,8]{1,4,3,2,0:T(8,128)(2,1)S(1)}, bf16[2,64,4,8,8]{1,4,3,2,0:T(8,128)(2,1)}, u32[]{:S(2)}) copy-start(bf16[2,64,4,8,8]{1,4,3,2,0:T(8,128)(2,1)} %param.24) | copy-start | bytes 196612
  20.1 7.2 %all-to-all-start = ((bf16[4,2,4096]{2,1,0:T(2,128)(2,1)}), bf16[4,2,4096]{2,1,0:T(2,128)(2,1)S(1)}, u32[]{:S(2)}, u32[]{:S(2)}) async-start(bf16[4,2,4096]{2,1,0:T(2,128)(2,1)} %reshape.373), calls=%async_computation | async-start | bytes 131072 | tf_op jit(solution)/shard_map/all_to_all | solution.py:73
  26.1 6.8 %copy-start.18 = (pred[32,16]{1,0:T(8,128)(4,1)}, pred[32,16]{1,0:T(8,128)(4,1)S(1)}, u32[]{:S(2)}) copy-start(pred[32,16]{1,0:T(8,128)(4,1)S(1)} %copy.271) | copy-start | bytes 1540
  43.3 4.3 %copy-start.19 = (pred[32,16]{1,0:T(8,128)(4,1)S(1)}, pred[32,16]{1,0:T(8,128)(4,1)}, u32[]{:S(2)}) copy-start(pred[32,16]{1,0:T(8,128)(4,1)} %copy-done.18) | copy-start | bytes 1540
  52.1 3.7 %copy-start.28 = (bf16[2,8,8,64]{3,2,1,0:T(8,128)(2,1)S(1)}, bf16[2,8,8,64]{3,2,1,0:T(8,128)(2,1)}, u32[]{:S(2)}) copy-start(bf16[2,8,8,64]{3,2,1,0:T(8,128)(2,1)} %param.25) | copy-start | bytes 49156
  55.8 2.7 copy-start.13
  55.8 2.8 copy-start.17
  57.4 11.4 %slice-start = ((bf16[2,32,32,128]{3,2,1,0:T(8,128)(2,1)}), bf16[1,32,32,128]{3,2,1,0:T(8,128)(2,1)S(1)}, s32[]{:S(2)}) async-start(bf16[2,32,32,128]{3,2,1,0:T(8,128)(2,1)} %param.27), calls=%async_computation.4 | async-start | bytes 524288 | tf_op jit(solution)/shard_map/slice | solution.py:77
  57.4 11.4 %copy-start.14 = (f32[32,128]{1,0:T(8,128)S(1)}, f32[32,128]{1,0:T(8,128)}, u32[]{:S(2)}) copy-start(f32[32,128]{1,0:T(8,128)} %convolution_add_fusion) | copy-start | bytes 49156
  68.8 4.2 %copy-start.20 = (bf16[2,128,4]{1,2,0:T(4,128)(2,1)S(1)}, bf16[2,128,4]{1,2,0:T(4,128)(2,1)}, u32[]{:S(2)}) copy-start(bf16[2,128,4]{1,2,0:T(4,128)(2,1)} %param.28) | copy-start | bytes 6148
  72.6 9.1 %copy-start.7 = (bf16[2,128,4,4,32]{1,4,3,2,0:T(8,128)(2,1)S(1)}, bf16[2,128,4,4,32]{1,4,3,2,0:T(8,128)(2,1)}, u32[]{:S(2)}) copy-start(bf16[2,128,4,4,32]{1,4,3,2,0:T(8,128)(2,1)} %param.29) | copy-start | bytes 786436
  84.9 8.0 %copy-start.34 = (pred[128]{0:T(512)(128)(4,1)S(1)}, pred[128]{0:T(512)(128)(4,1)}, u32[]{:S(2)}) copy-start(pred[128]{0:T(512)(128)(4,1)} %broadcast_compare_fusion) | copy-start | bytes 388
  89.4 35.2 %all-to-all-start.1 = ((bf16[4,2,4096]{2,1,0:T(2,128)(2,1)}), bf16[4,2,4096]{2,1,0:T(2,128)(2,1)S(1)}, u32[]{:S(2)}, u32[]{:S(2)}) async-start(bf16[4,2,4096]{2,1,0:T(2,128)(2,1)} %reshape.375), calls=%async_computation.1 | async-start | bytes 131072 | tf_op jit(solution)/shard_map/all_to_all | solution.py:91
  93.0 12.5 %copy-start.26 = (bf16[2,4,32,128]{3,2,1,0:T(8,128)(2,1)S(1)}, bf16[2,4,32,128]{3,2,1,0:T(8,128)(2,1)}, u32[]{:S(2)}) copy-start(bf16[2,4,32,128]{3,2,1,0:T(8,128)(2,1)} %param.30) | copy-start | bytes 196612
  124.7 4.9 %copy-start.11 = (bf16[2,64,4,8,8]{1,4,3,2,0:T(8,128)(2,1)S(1)}, bf16[2,64,4,8,8]{1,4,3,2,0:T(8,128)(2,1)}, u32[]{:S(2)}) copy-start(bf16[2,64,4,8,8]{1,4,3,2,0:T(8,128)(2,1)} %param.22) | copy-start | bytes 196612
  124.7 18.1 %all-to-all-start.2 = ((bf16[32,128,128]{2,0,1:T(8,128)(2,1)}), bf16[32,128,128]{2,0,1:T(8,128)(2,1)S(1)}, u32[]{:S(2)}, u32[]{:S(2)}) async-start(bf16[32,128,128]{2,0,1:T(8,128)(2,1)} %copy.297), calls=%async_computation.2 | async-start | bytes 2097152 | tf_op jit(solution)/shard_map/all_to_all | solution.py:81
  148.2 4.6 %copy-start = (bf16[128,32,4,4,32]{0,4,3,2,1:T(8,128)(2,1)}, bf16[128,32,4,4,32]{0,4,3,2,1:T(8,128)(2,1)S(1)}, u32[]{:S(2)}) copy-start(bf16[128,32,4,4,32]{0,4,3,2,1:T(8,128)(2,1)S(1)} %convolution_convert_fusion.2) | copy-start | bytes 12582916
  148.3 4.5 %copy-start.24 = (bf16[2,128,4]{1,2,0:T(4,128)(2,1)S(1)}, bf16[2,128,4]{1,2,0:T(4,128)(2,1)}, u32[]{:S(2)}) copy-start(bf16[2,128,4]{1,2,0:T(4,128)(2,1)} %param.31) | copy-start | bytes 6148
  179.9 6.1 %copy-start.15 = (f32[32,128]{1,0:T(8,128)S(1)}, f32[32,128]{1,0:T(8,128)}, u32[]{:S(2)}) copy-start(f32[32,128]{1,0:T(8,128)} %convolution_add_fusion) | copy-start | bytes 49156
  186.0 5.2 %copy-start.25 = (bf16[2,128,4]{1,2,0:T(4,128)(2,1)S(1)}, bf16[2,128,4]{1,2,0:T(4,128)(2,1)}, u32[]{:S(2)}) copy-start(bf16[2,128,4]{1,2,0:T(4,128)(2,1)} %param.31) | copy-start | bytes 6148
  203.9 2.9 %copy-start.35 = (pred[128]{0:T(512)(128)(4,1)S(1)}, pred[128]{0:T(512)(128)(4,1)}, u32[]{:S(2)}) copy-start(pred[128]{0:T(512)(128)(4,1)} %broadcast_compare_fusion) | copy-start | bytes 388
  218.6 5.4 %copy-start.16 = (f32[128,32]{0,1:T(8,128)S(1)}, f32[128,32]{0,1:T(8,128)}, u32[]{:S(2)}) copy-start(f32[128,32]{0,1:T(8,128)} %get-tuple-element.30) | copy-start | bytes 49156
  220.3 4.1 %copy-start.32 = (bf16[2,128,8]{1,2,0:T(8,128)(2,1)S(1)}, bf16[2,128,8]{1,2,0:T(8,128)(2,1)}, u32[]{:S(2)}) copy-start(bf16[2,128,8]{1,2,0:T(8,128)(2,1)} %param.21) | copy-start | bytes 12292
  220.3 26.3 %all-to-all-start.3 = ((bf16[128,32,128]{2,1,0:T(8,128)(2,1)}), bf16[128,32,128]{2,1,0:T(8,128)(2,1)S(1)}, u32[]{:S(2)}, u32[]{:S(2)}) async-start(bf16[128,32,128]{2,1,0:T(8,128)(2,1)} %copy.319), calls=%async_computation.3 | async-start | bytes 2097152 | tf_op jit(solution)/shard_map/all_to_all | solution.py:96
  223.9 17.6 %copy-start.23 = (pred[4,128]{1,0:T(4,128)(4,1)S(1)}, pred[4,128]{1,0:T(4,128)(4,1)}, u32[]{:S(2)}) copy-start(pred[4,128]{1,0:T(4,128)(4,1)} %copy-done.22) | copy-start | bytes 1540
  251.2 4.6 %copy-start.1 = (bf16[32,128,4,4,32]{1,4,3,2,0:T(8,128)(2,1)}, bf16[32,128,4,4,32]{1,4,3,2,0:T(8,128)(2,1)S(1)}, u32[]{:S(2)}) copy-start(bf16[32,128,4,4,32]{1,4,3,2,0:T(8,128)(2,1)S(1)} %convolution_convert_fusion) | copy-start | bytes 12582916
  251.3 4.6 %copy-start.21 = (bf16[2,128,4]{1,2,0:T(4,128)(2,1)S(1)}, bf16[2,128,4]{1,2,0:T(4,128)(2,1)}, u32[]{:S(2)}) copy-start(bf16[2,128,4]{1,2,0:T(4,128)(2,1)} %param.28) | copy-start | bytes 6148
  265.8 12.5 %copy-start.27 = (bf16[2,4,32,128]{3,2,1,0:T(8,128)(2,1)S(1)}, bf16[2,4,32,128]{3,2,1,0:T(8,128)(2,1)}, u32[]{:S(2)}) copy-start(bf16[2,4,32,128]{3,2,1,0:T(8,128)(2,1)} %param.30) | copy-start | bytes 196612
  (10 other events, 18.6 us)
where the time goes:
time: 289 us; the launch traced here: 285 us
  matrix products  87.6 us (30%)
  blocking collectives  80.2 us (28%)
  other arithmetic  56.9 us (20%)
  local copies, waits for them, and re-layouts  29.4 us (10%)
  starting transfers between devices  14.8 us (5%)
  waiting for transfers between devices  14.1 us (5%)
    sub x4, other arithmetic, gated_attention(): attn_probs = jax.nn.softmax(logits, axis=-1).astype(jnp.bfloat16)  44.5 us
    dot_general x8, matrix products, gated_attention(): jnp.einsum('abhd,hdc->abc', gated, w_out, preferred_element_type=jnp.floa...  31.5 us
    all_gather x1, blocking collectives, local_step(): lax.all_gather(pair_bias(layer_norm(pair_blk), w_row_bias[1], 'ijc,ch->hi...  16.8 us
    sub x4, matrix products, gated_attention(): attn_probs = jax.nn.softmax(logits, axis=-1).astype(jnp.bfloat16)  13.6 us
    all_to_all x1, waiting for transfers between devices, local_step(): pair_blk = lax.all_to_all(pair_blk, 'dap', 1, 0, tiled=True)  12.9 us
    all_gather x1, blocking collectives, local_step(): lax.all_gather(pair_bias(layer_norm(pair_blk), w_row_bias[0], 'ijc,ch->hi...  10.8 us
    all_gather x1, blocking collectives, local_step(): left_full = lax.all_gather(left, 'dap', axis=1, tiled=True)  10.5 us
    all_gather x1, blocking collectives, local_step(): right_full = lax.all_gather(right, 'dap', axis=1, tiled=True)  9.31 us
  transfers between devices with their start and end apart: 4, of which 2 were waited for; matrix products, arithmetic and copies ran while one was open for 11% of the time, Pallas kernels for 0%

commit v1 on v0

v1 whole, which is shorter than its diff:
```python
import functools

import jax
import jax.numpy as jnp
from jax import lax
from jax.experimental import pallas as pl
from jax.experimental.pallas import tpu as pltpu
from jax.sharding import PartitionSpec as P

F32 = jnp.float32
BF16 = jnp.bfloat16
LOG2E = 1.4426950408889634
NEG = -1e9 * LOG2E
N_DAP = 4
L = 128
R = 32
S = 16
C = 64
H = 8
L2 = 2 * L
MESH = pl.DeviceIdType.MESH


def mm(lhs, rhs):
    return jnp.dot(lhs, rhs, preferred_element_type=F32)


def mm_nt(lhs, rhs):
    return lax.dot_general(lhs, rhs, (((1,), (1,)), ((), ())), preferred_element_type=F32)


def lanes(parts):
    return jnp.concatenate(parts, axis=1)


def subl(parts):
    return jnp.concatenate(parts, axis=0)


def lo(x):
    return x[:, :L]


def hi(x):
    return x[:, L:]


def part(x, k, size):
    return x[k * size:(k + 1) * size]


def cols(k, size=L):
    return slice(k * size, (k + 1) * size)


def rows_at(n, size):
    return pl.ds(pl.multiple_of(n * size, size), size)


def pair(ref, n):
    return lanes([ref[n], ref[n + 1]])


def put_pair(ref, n, value):
    ref[n] = lo(value)
    ref[n + 1] = hi(value)


def only(value, k, size, count):
    zero = jnp.zeros((size, value.shape[1]), value.dtype)
    return subl([value if j == k else zero for j in range(count)])


def eye_bf16(n):
    rows = lax.broadcasted_iota(jnp.int32, (n, n), 0)
    columns = lax.broadcasted_iota(jnp.int32, (n, n), 1)
    return jnp.where(rows == columns, 1.0, 0.0).astype(BF16)


def layer_norm_t(x):
    x = x.astype(F32)
    inv_n = 1.0 / x.shape[0]
    centered = x - jnp.sum(x, axis=0, keepdims=True) * inv_n
    var = jnp.sum(centered * centered, axis=0, keepdims=True) * inv_n
    return (centered * lax.rsqrt(var + 1e-5)).astype(BF16)


def sigmoid(x):
    return 0.5 * jnp.tanh(0.5 * x) + 0.5


def round_bf16(x):
    return x.astype(BF16).astype(F32)


def pipeline(stages, trips):
    depth = len(stages)

    def run(t, first, last):
        for k in reversed(range(first, last)):
            stages[k](t - k)

    for t in range(depth - 1):
        run(t, 0, t + 1)

    def step(t, carry):
        run(t, 0, depth)
        return carry
    lax.fori_loop(depth - 1, trips, step, 0)
    for t in range(depth - 1):
        run(trips + t, t + 1, depth)


def body(
    m_in, z_in, msk, rmsk, w_bias, w_row_in, w_row_out, w_col_in, w_col_out, w_opm_in, w_opm_out,
    w_ts_in, w_ts_out, w_te_in, w_te_out,
    m_out, z_out,
    z_t, ln_t, p_q, p_kt, p_v, p_sg, k_s, bsc_row, bsc_tri, rb, tb, bt_row, bt_tri, m_all, ln_m, cp, og, cmask, kcols,
    mq, mkt, mv, acs, r_all, x_loc, o_scr, u_opm, z_snd, z_rcv, z_f, nrm, tmp, wro_t, wci_p, wco_t, woo_t, wtri_t,
    x_s, m_s, w_s, g_s,
    g_send, g_recv, a_send, a_recv,
):
    me = lax.axis_index('dap')
    data = lax.axis_index('data')
    my_rows = rows_at(me, R)

    def peer(o):
        return (data, lax.rem(me + o, N_DAP))

    barrier = pltpu.get_barrier_semaphore()
    for o in range(1, N_DAP):
        pl.semaphore_signal(barrier, inc=1, device_id=peer(o), device_id_type=MESH)
    pl.semaphore_wait(barrier, N_DAP - 1)

    def gather(stage, ref):
        return [
            pltpu.make_async_remote_copy(
                src_ref=ref, dst_ref=ref, send_sem=g_send.at[stage, o - 1], recv_sem=g_recv.at[stage, o - 1],
                device_id=peer(o), device_id_type=MESH)
            for o in range(1, N_DAP)
        ]

    def start(copies):
        for c in copies:
            c.start()

    def wait(copies):
        for c in copies:
            c.wait()

    def z_copy(stage, o, first, count):
        dest = lax.rem(me + o, N_DAP)
        return pltpu.make_async_remote_copy(
            src_ref=z_snd.at[stage, pl.ds(first, count), rows_at(dest, R), :],
            dst_ref=z_rcv.at[stage, pl.ds(me * R + first, count), :, :],
            send_sem=a_send.at[stage, o - 1], recv_sem=a_recv.at[stage, o - 1],
            device_id=(data, dest), device_id_type=MESH)

    e_c = eye_bf16(C)
    e_l = eye_bf16(L)

    def every(first, count, stride):
        return tmp[pl.ds(first, count, stride=stride), :]

    for b in range(2):
        wro_t[b] = mm_nt(e_c, w_row_out[b]).astype(BF16)
        tmp[:4 * C, :C] = w_col_in[b].astype(F32)
        wci_p[b] = subl([every(f * C + d, H, H) for f in range(4) for d in range(H)])[:, :C].astype(BF16)
        tmp[:C, :C] = w_col_out[b].astype(F32)
        wco_t[b] = mm_nt(e_c, subl([every(d, H, H) for d in range(H)])[:, :C].astype(BF16)).astype(BF16)
        wtri_t[0, b] = mm_nt(e_l, w_ts_out[b]).astype(BF16)
        wtri_t[1, b] = mm_nt(e_l, w_te_out[b]).astype(BF16)
    tmp[...] = w_opm_out[0].astype(F32)
    woo_t[0] = mm_nt(e_l, subl([every(q, R, R) for q in range(R)]).astype(BF16)).astype(BF16)
    woo_t[1] = mm_nt(e_l, w_opm_out[1]).astype(BF16)

    def down(row):
        return jnp.transpose(jnp.broadcast_to(row, (L, L)))

    mask_f = msk[...].astype(F32)
    for s in range(S):
        cmask[s] = jnp.broadcast_to(mask_f[s:s + 1, :], (H, L))
    mask_t = jnp.transpose(subl([mask_f] * H)).astype(BF16)[:, :S]
    nrm[...] = 1.0 / (1e-3 + mm(mask_t, mask_f.astype(BF16)))
    key_row = rmsk[...].astype(F32)
    key_col = down(key_row)
    key_row2 = lanes([key_row, key_row])
    for s in range(4):
        kcols[s] = down(msk[pl.ds(4 * me + s, 1), :].astype(F32))

    def bias_rows(bsc, ln_ref, b, group):
        def stage(t):
            n = t * 2
            rows = part(mm(w_bias[b], pair(ln_ref, n)), group, H)
            bsc[rows_at(n, H), :] = lo(rows)
            bsc[rows_at(n + 1, H), :] = hi(rows)
        return stage

    def pack_bias(bsc, ref, first, heads):
        for h in range(heads):
            ref[h, my_rows, :] = bsc[pl.ds(first + h, R, stride=H), :].astype(BF16)

    def normalise(t):
        for n in (t * 2, t * 2 + 1):
            ln_t[n] = layer_norm_t(z_t[n])

    def make_tri_bias(ref):
        for h in range(4):
            t = jnp.transpose(ref[h].astype(F32)) * LOG2E
            bt_tri[:, cols(h)] = jnp.where(key_col > 0, t, NEG)

    def tri_project(w_in_ref):
        def project(t):
            n = t * 2
            ln2 = pair(ln_t, n)
            put_pair(p_q, n, mm(part(w_in_ref, 0, L), ln2).astype(BF16))
            k_s[...] = round_bf16(mm(part(w_in_ref, 1, L), ln2)) * key_row2
            put_pair(p_v, n, mm(part(w_in_ref, 2, L), ln2).astype(BF16))
            put_pair(p_sg, n, round_bf16(mm(part(w_in_ref, 3, L), ln2)))

        def turn(t):
            for r in range(2):
                p_kt[t * 2 + r] = jnp.transpose(k_s[:, cols(r)]).astype(BF16)
                p_sg[t * 2 + r] = sigmoid(p_sg[t * 2 + r])

        pipeline([project, turn], R // 2)

    def weigh(t):
        for k in range(4):
            for half in (cols(0), cols(1)):
                e = jnp.exp2(x_s[k, :, half] - m_s[k, :, half])
                w_s[k, :, half] = (e * (1.0 / jnp.sum(e, axis=0, keepdims=True))).astype(BF16)

    def put_score(k, x):
        x_s[k] = x
        m_s[k] = jnp.max(x, axis=0, keepdims=True)

    def tri_attend(w_out_t, finish):
        scale = R ** -0.5 * LOG2E

        def score(t):
            for r in range(2):
                q = p_q[t * 2 + r]
                kt = p_kt[t * 2 + r]
                for hp in range(2):
                    blocks = [only(part(q, h, R), h, R, 4) for h in (2 * hp, 2 * hp + 1)]
                    put_score(2 * r + hp, mm(kt, lanes(blocks)) * scale + bt_tri[:, cols(hp, L2)])

        def gather_values(t):
            for r in range(2):
                v = p_v[t * 2 + r]
                outs = []
                for hp in range(2):
                    o2 = mm(part(v, hp, C), w_s[2 * r + hp])
                    outs += [lo(part(o2, 0, R)), hi(part(o2, 1, R))]
                g_s[:, cols(r)] = (subl(outs) * p_sg[t * 2 + r]).astype(BF16)

        def project_out(t):
            finish[0](t, pair(z_t, t * 2).astype(F32) + mm(w_out_t[...], g_s[...]))

        pipeline([score, weigh, gather_values, project_out] + finish[1:], R // 2)

    def row_attention(b, load, store):
        scale = H ** -0.5 * LOG2E
        for t in range(4):
            proj = round_bf16(mm(w_row_in[b], layer_norm_t(load(t))))
            q, k, v, g = [part(proj, f, C) for f in range(4)]
            mq[t] = q
            mkt[t] = jnp.transpose(subl([k, k]))[:, :C].astype(BF16)
            mv[t] = v.astype(BF16)
            p_sg[t, :C] = sigmoid(g)

        def score(t):
            kt = mkt[t]
            kcol = kcols[t]
            kcol2 = lanes([kcol, kcol])
            for hp in range(4):
                blocks = [only(mq[t, cols(h, H)], h, H, H) for h in (2 * hp, 2 * hp + 1)]
                x = mm(kt, lanes(blocks).astype(BF16)) * scale + bt_row[:, cols(hp, L2)]
                put_score(hp, jnp.where(kcol2 > 0, x, NEG))

        def gather_values(t):
            outs = []
            for hp in range(4):
                o2 = mm(mv[t, cols(hp, S)], w_s[hp])
                outs += [lo(part(o2, 0, H)), hi(part(o2, 1, H))]
            g_s[:C, :L] = (subl(outs) * p_sg[t, :C]).astype(BF16)

        def project_out(t):
            store(t, (load(t).astype(F32) + mm(wro_t[b], g_s[:C, :L])).astype(BF16))

        pipeline([score, weigh, gather_values, project_out], 4)

    def col_attention(b):
        scale = H ** -0.5 * LOG2E

        def normalise_m(t):
            for s in (2 * t, 2 * t + 1):
                ln_m[s] = layer_norm_t(m_all[s])

        def project(t):
            proj = round_bf16(mm(wci_p[b], pair(ln_m, 2 * t)))
            put_pair(cp, 2 * t, subl([proj[:3 * C], sigmoid(part(proj, 3, C))]))
        pipeline([normalise_m, project], S // 2)

        def attend(a, carry):
            def at(s, f, d):
                return cp[s, cols(f * H + d, H)]

            q = [at(a, 0, d) for d in range(H)]
            logits = []
            for t in range(S):
                acc = functools.reduce(jnp.add, [q[d] * at(t, 1, d) for d in range(H)])
                logits.append(jnp.where(cmask[t] > 0, acc * scale, NEG))
            top = functools.reduce(jnp.maximum, logits)
            e = [jnp.exp2(x - top) for x in logits]
            inv = 1.0 / functools.reduce(jnp.add, e)
            probs = [round_bf16(x * inv) for x in e]
            outs = [functools.reduce(jnp.add, [probs[t] * at(t, 2, d) for t in range(S)]) for d in range(H)]
            og[a] = (subl(outs) * cp[a, cols(3, C)]).astype(BF16)
            return carry
        lax.fori_loop(0, S, attend, 0)

        def update(t):
            new = pair(m_all, 2 * t).astype(F32) + mm(wco_t[b], pair(og, 2 * t))
            put_pair(m_all, 2 * t, new.astype(BF16))

        def halves(t):
            both = mm(w_opm_in[b], pair(ln_m, 2 * t))
            for s, x in ((2 * t, lo(both)), (2 * t + 1, hi(both))):
                acs[rows_at(s, C), :] = x * msk[pl.ds(s, 1), :].astype(F32)
        pipeline([update, normalise_m, halves], S // 2)

    row_id = lax.broadcasted_iota(jnp.int32, (S, L2), 0)
    lane_id = lax.broadcasted_iota(jnp.int32, (S, L2), 1)
    diag = row_id == lane_id // S

    def opm(b, finish):
        local, other = (0, R) if b == 0 else (R, 0)
        for q in range(R):
            r_all[q] = acs[pl.ds(other + q, S, stride=C), :].astype(BF16)
        for t in range(4):
            rows = subl([acs[pl.ds(local + H * t + p, S, stride=C), :] for p in range(H)])
            x_loc[:, cols(t)] = jnp.transpose(round_bf16(rows))

        def outer(t):
            left = []
            for k in range(4):
                row = x_loc[pl.ds(me * R + t * 4 + k, 1), :]
                for half in (cols(0, L2), cols(1, L2)):
                    left.append(jnp.where(diag, jnp.broadcast_to(row[:, half], (S, L2)), 0.0))
            left = subl(left).astype(BF16)
            for q in range(0, R, 2):
                put_pair(o_scr, q, mm(left, lanes([subl([r_all[q]] * S), subl([r_all[q + 1]] * S)])).astype(BF16))

        def contract(t):
            for k in range(2):
                blocks = [o_scr[:, cols(2 * k + j, R), :].reshape(R * R, L) for j in range(2)]
                n = t * 4 + 2 * k
                at = me * R + n
                norm = lanes([nrm[pl.ds(at, 1), :], nrm[pl.ds(at + 1, 1), :]])
                finish[0](n, mm(woo_t[b], lanes(blocks)) * norm)

        pipeline([outer, contract] + [
            lambda t, f=f: (f(2 * t), f(2 * t + 1)) for f in finish[1:]], R // 4)

    def put_z(t, z2):
        put_pair(z_t, 2 * t, z2.astype(BF16))

    def send_z(stage):
        def turn(t, z2):
            z2 = round_bf16(z2)
            for r, x in ((0, lo(z2)), (1, hi(z2))):
                z_snd[stage, 2 * t + r] = jnp.transpose(x).astype(BF16)

        def send(t):
            for o in range(1, N_DAP):
                z_copy(stage, o, 2 * t, 2).start()
            for n in (2 * t, 2 * t + 1):
                z_rcv[stage, me * R + n] = z_snd[stage, n, my_rows, :]
        return [turn, send]

    def receive_z(stage, b):
        for o in range(1, N_DAP):
            z_copy(stage, o, 0, R).wait()

        def widen(t):
            for r in range(4):
                n = t * 4 + r
                z_f[pl.ds(pl.multiple_of(n * (R + H), H), R), :] = z_rcv[stage, n].astype(F32)
        pipeline([widen], R)

        def turn(t):
            for n in (2 * t, 2 * t + 1):
                z_t[n] = jnp.transpose(z_f[pl.ds(n, L, stride=R + H), :]).astype(BF16)
        pipeline([turn, normalise, bias_rows(bsc_tri, ln_t, b, 1)], R // 2)

    def enter(t):
        for n in (2 * t, 2 * t + 1):
            z_t[n] = jnp.transpose(z_in[n].astype(F32)).astype(BF16)
    pipeline([enter, normalise, bias_rows(bsc_row, ln_t, 0, 0)], R // 2)
    pack_bias(bsc_row, rb.at[0], 0, H)
    g = gather(0, rb.at[0, :, my_rows, :])
    start(g)
    wait(g)
    for h in range(H):
        bt_row[:, cols(h)] = jnp.transpose(rb[0, h].astype(F32)) * LOG2E

    def store_m(s, value):
        m_all[4 * me + s] = value
    row_attention(0, lambda s: m_in[s], store_m)
    g = gather(1, m_all.at[pl.ds(4 * me, 4)])
    start(g)
    wait(g)
    col_attention(0)

    def add_first(n, update2):
        put_pair(z_t, n, (pair(z_t, n).astype(F32) + update2).astype(BF16))
    opm(0, [add_first, normalise, bias_rows(bsc_tri, ln_t, 0, 1)])
    pack_bias(bsc_tri, tb.at[0], 0, 4)
    g = gather(2, tb.at[0, :, my_rows, :])
    start(g)
    tri_project(w_ts_in.at[0])
    wait(g)
    make_tri_bias(tb.at[0])
    tri_attend(wtri_t.at[0, 0], send_z(0))

    col_attention(1)

    def keep_update(n, update2):
        put_pair(u_opm, n, update2)
    opm(1, [keep_update])

    receive_z(0, 0)
    pack_bias(bsc_tri, tb.at[1], 4, 4)
    g = gather(3, tb.at[1, :, my_rows, :])
    start(g)
    tri_project(w_te_in.at[0])
    wait(g)
    make_tri_bias(tb.at[1])
    tri_attend(wtri_t.at[1, 0], [put_z, normalise, bias_rows(bsc_row, ln_t, 1, 0)])

    pack_bias(bsc_row, rb.at[1], 0, H)
    g_row = gather(4, rb.at[1, :, my_rows, :])
    start(g_row)

    def add_second(t):
        put_z(t, pair(z_t, 2 * t).astype(F32) + pair(u_opm, 2 * t))
    pipeline([add_second, normalise, bias_rows(bsc_tri, ln_t, 1, 1)], R // 2)
    pack_bias(bsc_tri, tb.at[2], 4, 4)
    g = gather(5, tb.at[2, :, my_rows, :])
    start(g)
    tri_project(w_te_in.at[1])
    wait(g)
    make_tri_bias(tb.at[2])
    tri_attend(wtri_t.at[1, 1], send_z(1))

    wait(g_row)
    for h in range(H):
        bt_row[:, cols(h)] = rb[1, h].astype(F32) * LOG2E

    def emit_m(s, value):
        m_out[s] = value
    row_attention(1, lambda s: m_all[4 * me + s], emit_m)

    receive_z(1, 1)
    pack_bias(bsc_tri, tb.at[3], 0, 4)
    g = gather(6, tb.at[3, :, my_rows, :])
    start(g)
    tri_project(w_ts_in.at[1])
    wait(g)
    make_tri_bias(tb.at[3])

    def emit_z(t, z2):
        for n, x in ((2 * t, lo(z2)), (2 * t + 1, hi(z2))):
            z_out[n] = jnp.transpose(x).astype(BF16)
    tri_attend(wtri_t.at[0, 1], [emit_z])


def solution(mesh):
    def local_step(msa_act, pair_act, msa_mask, res_mask, w_row_bias, w_row_in, w_row_out, w_col_in, w_col_out, w_opm_in, w_opm_out, w_ts_bias, w_ts_in, w_ts_out, w_te_bias, w_te_in, w_te_out):
        def rows_first(w):
            w = jnp.moveaxis(w, 1, -1)
            return w.reshape(2, -1, w.shape[-1])

        def flat_out(w):
            return w.reshape(2, -1, w.shape[-1])

        w_bias = jnp.concatenate([jnp.swapaxes(w, 1, 2) for w in (w_row_bias, w_ts_bias, w_te_bias)], axis=1)
        vmem = pl.BlockSpec(memory_space=pltpu.VMEM)

        def wide(*shape):
            return pltpu.VMEM(shape, F32)

        def half(*shape):
            return pltpu.VMEM(shape, BF16)

        scratch = dict(
            z_t=half(R, L, L), ln_t=half(R, L, L), p_q=half(R, L, L), p_kt=half(R, L, L), p_v=half(R, L, L),
            p_sg=wide(R, L, L), k_s=wide(L, L2), bsc_row=wide(R * H, L), bsc_tri=wide(R * H, L),
            rb=half(2, H, L, L), tb=half(4, 4, L, L), bt_row=wide(L, H * L), bt_tri=wide(L, 4 * L),
            m_all=half(S, C, L), ln_m=half(S, C, L), cp=wide(S, 4 * C, L), og=half(S, C, L),
            cmask=wide(S, H, L), kcols=wide(4, L, L), mq=wide(4, C, L), mkt=half(4, L, C), mv=half(4, C, L),
            acs=wide(S * C, L), r_all=half(R, S, L), x_loc=wide(L, R * S),
            o_scr=half(R, L, L), u_opm=wide(R, L, L), z_snd=half(2, R, L, L), z_rcv=half(2, L, R, L),
            z_f=wide(L * (R + H), L), nrm=wide(L, L), tmp=wide(R * R, L),
            wro_t=half(2, C, C), wci_p=half(2, 4 * C, C), wco_t=half(2, C, C), woo_t=half(2, L, R * R),
            wtri_t=half(2, 2, L, L), x_s=wide(4, L, L2), m_s=wide(4, 1, L2), w_s=half(4, L, L2), g_s=half(L, L2),
        )
        sems = [pltpu.SemaphoreType.DMA((n, N_DAP - 1)) for n in (7, 7, 2, 2)]
        m_new, z_new = pl.pallas_call(
            body,
            out_shape=(jax.ShapeDtypeStruct((4, C, L), BF16), jax.ShapeDtypeStruct((R, L, L), BF16)),
            in_specs=[vmem] * 15,
            out_specs=(vmem, vmem),
            scratch_shapes=list(scratch.values()) + sems,
            compiler_params=pltpu.CompilerParams(collective_id=0, has_side_effects=True, vmem_limit_bytes=60 * 2 ** 20),
        )(
            jnp.swapaxes(msa_act, 1, 2), pair_act, msa_mask, res_mask.reshape(1, L), w_bias,
            rows_first(w_row_in), flat_out(w_row_out), rows_first(w_col_in), flat_out(w_col_out),
            rows_first(w_opm_in), flat_out(w_opm_out),
            rows_first(w_ts_in), flat_out(w_ts_out), rows_first(w_te_in), flat_out(w_te_out),
        )
        return jnp.swapaxes(m_new, 1, 2), z_new

    in_specs = (P(('data', 'dap')), P(('data', 'dap')), P('data'), P('data')) + (P(),) * 13
    out_specs = (P(('data', 'dap')), P(('data', 'dap')))
    return jax.shard_map(local_step, mesh=mesh, in_specs=in_specs, out_specs=out_specs, check_vma=False)
```

time: 289 us -> 98.3 us (0.34); the launches traced: 285 us -> 98 us
  Pallas kernels: 0 us -> 92.3 us
  matrix products: 87.6 us -> 0 us
  blocking collectives: 80.2 us -> 0 us
  other arithmetic: 56.9 us -> 0.61 us
  local copies, waits for them, and re-layouts: 29.4 us -> 4.47 us
  starting transfers between devices: 14.8 us -> 0 us
  waiting for transfers between devices: 14.1 us -> 0 us
    pallas_call x0 -> x1, Pallas kernels: none -> 92.3 us  [local_step(): pl.pallas_call(body, out_shape=(jax.ShapeDtypeStruct((4, C, L), BF16), ja...]
    all_gather x8 -> x0, blocking collectives: 80.2 us -> none  [the longest x1 16.8 us: local_step(): lax.all_gather(pair_bias(layer_norm(pair_blk), w_row_bias[1], 'ijc,ch->hi...]
    dot_general x33 -> x0, matrix products: 74 us -> none  [the longest x8 31.5 us: gated_attention(): jnp.einsum('abhd,hdc->abc', gated, w_out, preferred_element_type=jnp.floa...]
    sub x4 -> x0, other arithmetic: 44.5 us -> none  [gated_attention(): attn_probs = jax.nn.softmax(logits, axis=-1).astype(jnp.bfloat16)]
    all_to_all x4 -> x0, starting transfers between devices: 14.8 us -> none  [the longest x1 3.91 us: local_step(): pair_blk = lax.all_to_all(pair_blk, 'dap', 1, 0, tiled=True)]
    all_to_all x4 -> x0, waiting for transfers between devices: 14.1 us -> none  [the longest x1 12.9 us: local_step(): pair_blk = lax.all_to_all(pair_blk, 'dap', 1, 0, tiled=True)]
    sub x4 -> x0, matrix products: 13.6 us -> none  [gated_attention(): attn_probs = jax.nn.softmax(logits, axis=-1).astype(jnp.bfloat16)]
    convert_element_type x19 -> x0, local copies, waits for them, and re-layouts: 9.74 us -> none  [the longest x9 7.97 us: add_residual(): return (current.astype(jnp.float32) + update).astype(jnp.bfloat16)]
  transfers between devices with their start and end apart: 4 -> 0, of which waited for: 2 -> 0; matrix products, arithmetic and copies ran while one was open for 11% -> 0% of each run, Pallas kernels for 0% -> 0%
where the time goes in v1:
time: 98.3 us; the launch traced here: 98 us
  Pallas kernels  92.3 us (94%)
  local copies, waits for them, and re-layouts  4.47 us (5%)
    pallas_call x1, Pallas kernels, local_step(): pl.pallas_call(body, out_shape=(jax.ShapeDtypeStruct((4, C, L), BF16), ja...  92.3 us
    unnamed x8, local copies, waits for them, and re-layouts  4.47 us

profile of v1, /device:TPU:0, one launch (start us, length us, event | category | flops | bytes accessed | tf_op | source)
XLA Modules:
  0.0 98.0 jit_solution(15280869774181772059)
XLA Ops:
  0.6 0.0 copy-start.2
  0.6 0.0 copy-start
  0.7 0.0 copy-start.1
  0.7 0.7 copy-done.2
  1.3 0.0 copy-done
  1.3 0.0 copy-done.1
  1.3 0.6 pad_maximum_fusion.w_bias
  2.0 92.3 %shard_map.176 = (bf16[4,64,128]{2,1,0:T(8,128)(2,1)}, bf16[32,128,128]{2,1,0:T(8,128)(2,1)}) custom-call(bf16[4,64,128]{2,1,0:T(8,128)(2,1)} %bitcast.31, bf16[32,128,128]{2,1,0:T(8,128)(2,1)} %z_in.1, s32[16,128]{1,0:T(8,128)} %msk.1, s32[1,128]{1,0:T(1,128)} %bitcast.41, bf16[2,16,128]{2,1,0:T(8,128)(2,1)} %pad_maximum_fusion.w_bias, ...), custom_call_target="tpu_custom_call" | custom-call | tf_op jit(solution)/shard_map/pallas_call | solution.py:511
  94.2 1.5 %copy.21 = bf16[4,128,64]{1,2,0:T(8,128)(2,1)} copy(bf16[4,128,64]{1,2,0:T(8,128)(2,1)} %bitcast.34) | data formatting | bytes 131072
  95.7 2.3 %copy.22 = bf16[32,128,128]{2,1,0:T(8,128)(2,1)} copy(bf16[32,128,128]{2,1,0:T(8,128)(2,1)} %get-tuple-element.9) | data formatting | bytes 2097152
Async XLA Ops:
  0.6 0.7 copy-start.2
  0.6 0.7 copy-start
  0.7 0.7 copy-start.1

commit v2 on v1

--- a/solution.py
+++ b/solution.py
@@ -12,6 +12,7 @@
 LOG2E = 1.4426950408889634
 NEG = -1e9 * LOG2E
 N_DAP = 4
+N_IN = 15
 L = 128
 R = 32
 S = 16
@@ -93,30 +94,40 @@
     return x.astype(BF16).astype(F32)
 
 
-def pipeline(stages, trips):
+def pipeline(stages, trips, pause=None, resume=None):
     depth = len(stages)
 
     def run(t, first, last):
         for k in reversed(range(first, last)):
             stages[k](t - k)
 
-    for t in range(depth - 1):
-        run(t, 0, t + 1)
-
     def step(t, carry):
         run(t, 0, depth)
         return carry
-    lax.fori_loop(depth - 1, trips, step, 0)
+
+    for t in range(depth - 1):
+        run(t, 0, t + 1)
+    if pause is not None:
+        lax.fori_loop(depth - 1, pause, step, 0)
+        resume()
+    lax.fori_loop(depth - 1 if pause is None else pause, trips, step, 0)
     for t in range(depth - 1):
         run(trips + t, t + 1, depth)
 
 
 def body(
-    m_in, z_in, msk, rmsk, w_bias, w_row_in, w_row_out, w_col_in, w_col_out, w_opm_in, w_opm_out,
-    w_ts_in, w_ts_out, w_te_in, w_te_out,
-    m_out, z_out,
-    z_t, ln_t, p_q, p_kt, p_v, p_sg, k_s, bsc_row, bsc_tri, rb, tb, bt_row, bt_tri, m_all, ln_m, cp, og, cmask, kcols,
-    mq, mkt, mv, acs, r_all, x_loc, o_scr, u_opm, z_snd, z_rcv, z_f, nrm, tmp, wro_t, wci_p, wco_t, woo_t, wtri_t,
+    m_hbm, *refs,
+):
+    n = N_IN - 1
+    given, (m_out, z_out), refs = refs[:n], refs[n:n + 2], refs[n + 2:]
+    held, in_sems, refs = refs[:n], refs[n], refs[n + 1:]
+    main(m_hbm, given, held, in_sems, m_out, z_out, *refs)
+
+
+def main(
+    m_hbm, given, held, in_sems, m_out, z_out,
+    z_t, ln_t, p_q, p_kt, p_v, p_sg, k_s, bsc_row, bsc_tri, rb, tb, bt_row, bt_tri, m_all, m_dev, m_own, ln_m, cq, ckv, og,
+    cmask, omask, kcols, mq, mkt, mv, pick, spread, join, acs, r_all, x_loc, o_scr, u_opm, z_snd, z_rcv, z_f, nrm, tmp, wro_t, wci_p, wco_t, woo_t, wtri_t,
     x_s, m_s, w_s, g_s,
     g_send, g_recv, a_send, a_recv,
 ):
@@ -126,6 +137,15 @@
 
     def peer(o):
         return (data, lax.rem(me + o, N_DAP))
+
+    z_in, msk, rmsk, w_bias, w_row_in, w_row_out, w_col_in, w_col_out, w_opm_in, w_opm_out = held[:10]
+    w_ts_in, w_ts_out, w_te_in, w_te_out = held[10:]
+    own_m = m_all.at[pl.ds(4 * me, 4)]
+    copy_m = pltpu.make_async_copy(m_hbm, own_m, in_sems.at[N_IN - 1])
+    copy_m.start()
+    copies_in = [pltpu.make_async_copy(src, dst, in_sems.at[k]) for k, (src, dst) in enumerate(zip(given, held))]
+    for c in copies_in:
+        c.start()
 
     barrier = pltpu.get_barrier_semaphore()
     for o in range(1, N_DAP):
@@ -148,13 +168,19 @@
         for c in copies:
             c.wait()
 
-    def z_copy(stage, o, first, count):
+    def z_copy(stage, o, first, count, at=0, size=R):
         dest = lax.rem(me + o, N_DAP)
         return pltpu.make_async_remote_copy(
-            src_ref=z_snd.at[stage, pl.ds(first, count), rows_at(dest, R), :],
-            dst_ref=z_rcv.at[stage, pl.ds(me * R + first, count), :, :],
+            src_ref=z_snd.at[min(stage, 1), pl.ds(first, count), pl.ds(pl.multiple_of(dest * R + at, S), size), :],
+            dst_ref=z_rcv.at[min(stage, 1), pl.ds(me * R + first, count), pl.ds(at, size), :],
             send_sem=a_send.at[stage, o - 1], recv_sem=a_recv.at[stage, o - 1],
             device_id=(data, dest), device_id_type=MESH)
+
+    copy_m.wait()
+    g_in = gather(0, own_m)
+    start(g_in)
+    for c in copies_in:
+        c.wait()
 
     e_c = eye_bf16(C)
     e_l = eye_bf16(L)
@@ -168,11 +194,16 @@
         wci_p[b] = subl([every(f * C + d, H, H) for f in range(4) for d in range(H)])[:, :C].astype(BF16)
         tmp[:C, :C] = w_col_out[b].astype(F32)
         wco_t[b] = mm_nt(e_c, subl([every(d, H, H) for d in range(H)])[:, :C].astype(BF16)).astype(BF16)
-        wtri_t[0, b] = mm_nt(e_l, w_ts_out[b]).astype(BF16)
-        wtri_t[1, b] = mm_nt(e_l, w_te_out[b]).astype(BF16)
-    tmp[...] = w_opm_out[0].astype(F32)
-    woo_t[0] = mm_nt(e_l, subl([every(q, R, R) for q in range(R)]).astype(BF16)).astype(BF16)
-    woo_t[1] = mm_nt(e_l, w_opm_out[1]).astype(BF16)
+
+    def late_weights():
+        for b in range(2):
+            wtri_t[0, b] = mm_nt(e_l, w_ts_out[b]).astype(BF16)
+            wtri_t[1, b] = mm_nt(e_l, w_te_out[b]).astype(BF16)
+        tmp[...] = w_opm_out[0].astype(F32)
+        woo_t[0] = mm_nt(e_l, subl([every(q, R, R) for q in range(R)]).astype(BF16)).astype(BF16)
+        woo_t[1] = mm_nt(e_l, w_opm_out[1]).astype(BF16)
+        src, lane = iota((4 * L, 4 * L), 0), iota((4 * L, 4 * L), 1)
+        join[...] = ones_at((src // L == lane % L // R) & (src % L == lane // L * R + lane % R))
 
     def down(row):
         return jnp.transpose(jnp.broadcast_to(row, (L, L)))
@@ -185,8 +216,24 @@
     key_row = rmsk[...].astype(F32)
     key_col = down(key_row)
     key_row2 = lanes([key_row, key_row])
-    for s in range(4):
-        kcols[s] = down(msk[pl.ds(4 * me + s, 1), :].astype(F32))
+    turned = jnp.transpose(subl([mask_f] * H))
+    for s in range(S):
+        kcols[s] = jnp.broadcast_to(turned[:, s:s + 1], (L, L))
+
+    def iota(shape, axis):
+        return lax.broadcasted_iota(jnp.int32, shape, axis)
+
+    def ones_at(where):
+        return jnp.where(where, 1.0, 0.0).astype(BF16)
+
+    src, lane = iota((4 * L, L), 0), iota((4 * L, L), 1)
+    pick[...] = ones_at((src // L == lane // R) & (src % L == me * R + lane % R))
+    src, lane = iota((L, 8 * L), 0), iota((L, 8 * L), 1)
+    spread[...] = ones_at(src == lane // L2 * R + lane % R)
+    src, lane = iota((L, L), 0), iota((L, L), 1)
+    own_mask = mm(mask_f.astype(BF16), ones_at(src == me * R + lane % R))
+    for s in range(S):
+        omask[s] = jnp.broadcast_to(own_mask[s:s + 1, :], (H, L))
 
     def bias_rows(bsc, ln_ref, b, group):
         def stage(t):
@@ -204,12 +251,13 @@
         for n in (t * 2, t * 2 + 1):
             ln_t[n] = layer_norm_t(z_t[n])
 
-    def make_tri_bias(ref):
+    def make_tri_bias(ref, by_key):
         for h in range(4):
-            t = jnp.transpose(ref[h].astype(F32)) * LOG2E
+            t = ref[h].astype(F32) * LOG2E
+            t = t if by_key else jnp.transpose(t)
             bt_tri[:, cols(h)] = jnp.where(key_col > 0, t, NEG)
 
-    def tri_project(w_in_ref):
+    def project_stages(w_in_ref):
         def project(t):
             n = t * 2
             ln2 = pair(ln_t, n)
@@ -223,7 +271,7 @@
                 p_kt[t * 2 + r] = jnp.transpose(k_s[:, cols(r)]).astype(BF16)
                 p_sg[t * 2 + r] = sigmoid(p_sg[t * 2 + r])
 
-        pipeline([project, turn], R // 2)
+        return [project, turn]
 
     def weigh(t):
         for k in range(4):
@@ -235,7 +283,7 @@
         x_s[k] = x
         m_s[k] = jnp.max(x, axis=0, keepdims=True)
 
-    def tri_attend(w_out_t, finish):
+    def attend_stages(w_out_t, finish):
         scale = R ** -0.5 * LOG2E
 
         def score(t):
@@ -258,24 +306,24 @@
         def project_out(t):
             finish[0](t, pair(z_t, t * 2).astype(F32) + mm(w_out_t[...], g_s[...]))
 
-        pipeline([score, weigh, gather_values, project_out] + finish[1:], R // 2)
+        return [score, weigh, gather_values, project_out] + finish[1:]
 
     def row_attention(b, load, store):
         scale = H ** -0.5 * LOG2E
         for t in range(4):
             proj = round_bf16(mm(w_row_in[b], layer_norm_t(load(t))))
             q, k, v, g = [part(proj, f, C) for f in range(4)]
-            mq[t] = q
+            p_sg[4 + t, :C] = q
             mkt[t] = jnp.transpose(subl([k, k]))[:, :C].astype(BF16)
             mv[t] = v.astype(BF16)
             p_sg[t, :C] = sigmoid(g)
 
         def score(t):
             kt = mkt[t]
-            kcol = kcols[t]
+            kcol = kcols[4 * me + t]
             kcol2 = lanes([kcol, kcol])
             for hp in range(4):
-                blocks = [only(mq[t, cols(h, H)], h, H, H) for h in (2 * hp, 2 * hp + 1)]
+                blocks = [only(p_sg[4 + t, cols(h, H)], h, H, H) for h in (2 * hp, 2 * hp + 1)]
                 x = mm(kt, lanes(blocks).astype(BF16)) * scale + bt_row[:, cols(hp, L2)]
                 put_score(hp, jnp.where(kcol2 > 0, x, NEG))
 
@@ -291,45 +339,119 @@
 
         pipeline([score, weigh, gather_values, project_out], 4)
 
-    def col_attention(b):
+    same_head = iota((C, L2), 0) // H == iota((C, L2), 1) // R
+    block = iota((C, L), 1) // R
+
+    def row_attention_own():
         scale = H ** -0.5 * LOG2E
-
-        def normalise_m(t):
-            for s in (2 * t, 2 * t + 1):
-                ln_m[s] = layer_norm_t(m_all[s])
-
-        def project(t):
-            proj = round_bf16(mm(wci_p[b], pair(ln_m, 2 * t)))
-            put_pair(cp, 2 * t, subl([proj[:3 * C], sigmoid(part(proj, 3, C))]))
-        pipeline([normalise_m, project], S // 2)
+        rows = subl([bsc_row[pl.ds(h, R, stride=H), :] for h in range(H)])
+        bias = jnp.transpose(round_bf16(rows)) * LOG2E
+        bt_row[:, :L2] = bias
+        w_qg = subl([part(w_row_in[0], 0, C), part(w_row_in[0], 3, C)])
+
+        def keys(t):
+            ln2 = lanes([layer_norm_t(m_all[2 * t]), layer_norm_t(m_all[2 * t + 1])])
+            kv = round_bf16(mm(w_row_in[0, C:3 * C], ln2))
+            for s, x in ((2 * t, lo(kv)), (2 * t + 1, hi(kv))):
+                mkt[s] = jnp.transpose(x)[:, :C].astype(BF16)
+                mv[s] = part(x, 1, C).astype(BF16)
+
+        def queries(t):
+            own = mm(lanes([m_all[4 * t + k] for k in range(4)]), pick[...])
+            m_own[t] = own.astype(BF16)
+            qg = round_bf16(mm(w_qg, layer_norm_t(own)))
+            p_sg[t, :C] = sigmoid(part(qg, 1, C))
+            q = mm(part(qg, 0, C).astype(BF16), spread[...])
+            for k in range(4):
+                mq[4 * t + k] = jnp.where(same_head, q[:, cols(k, L2)], 0.0).astype(BF16)
+
+        def score(t):
+            for k in range(4):
+                s = 4 * t + k
+                x = mm(mkt[s], mq[s]) * scale + bt_row[:, :L2]
+                put_score(k, jnp.where(lanes([kcols[s], kcols[s]]) > 0, x, NEG))
+
+        def gather_values(t):
+            out = jnp.zeros((C, L), F32)
+            for k in range(4):
+                o2 = jnp.where(same_head, mm(mv[4 * t + k], w_s[k]), 0.0)
+                o = lo(o2) + hi(o2)
+                o = o + pltpu.roll(o, C, 1)
+                o = o + pltpu.roll(o, R, 1)
+                out = jnp.where(block == k, o, out)
+            g_s[:C, :L] = (out * p_sg[t, :C]).astype(BF16)
+
+        def project_out(t):
+            m_own[t] = (m_own[t].astype(F32) + mm(wro_t[0], g_s[:C, :L])).astype(BF16)
+
+        for t in range(4):
+            queries(t)
+        for t in range(S // 2):
+            keys(t)
+        pipeline([score, weigh, gather_values, project_out], 4)
+
+    def attend_columns(steps, mask):
+        scale = H ** -0.5 * LOG2E
 
         def attend(a, carry):
             def at(s, f, d):
-                return cp[s, cols(f * H + d, H)]
-
-            q = [at(a, 0, d) for d in range(H)]
+                return ckv[s, cols(f * H + d, H)]
+
+            q = [cq[a, cols(d, H)] for d in range(H)]
             logits = []
             for t in range(S):
-                acc = functools.reduce(jnp.add, [q[d] * at(t, 1, d) for d in range(H)])
-                logits.append(jnp.where(cmask[t] > 0, acc * scale, NEG))
+                acc = functools.reduce(jnp.add, [q[d] * at(t, 0, d) for d in range(H)])
+                logits.append(jnp.where(mask[t] > 0, acc * scale, NEG))
             top = functools.reduce(jnp.maximum, logits)
             e = [jnp.exp2(x - top) for x in logits]
             inv = 1.0 / functools.reduce(jnp.add, e)
             probs = [round_bf16(x * inv) for x in e]
-            outs = [functools.reduce(jnp.add, [probs[t] * at(t, 2, d) for t in range(S)]) for d in range(H)]
-            og[a] = (subl(outs) * cp[a, cols(3, C)]).astype(BF16)
+            outs = [functools.reduce(jnp.add, [probs[t] * at(t, 1, d) for t in range(S)]) for d in range(H)]
+            og[a] = (subl(outs) * part(cq[a], 1, C)).astype(BF16)
             return carry
-        lax.fori_loop(0, S, attend, 0)
+        lax.fori_loop(0, steps, attend, 0)
+
+    def col_attention_own():
+        ln4 = lanes([layer_norm_t(m_own[t]) for t in range(4)])
+        proj = round_bf16(mm(wci_p[0], ln4))
+        for t in range(4):
+            x = proj[:, cols(t)]
+            cq[t] = subl([part(x, 0, C), sigmoid(part(x, 3, C))])
+            kv = x[C:3 * C].astype(BF16)
+            for k in range(4):
+                ckv[4 * t + k] = mm(kv, spread[:, cols(2 * k)])
+        attend_columns(4, omask)
+        new = mm(wco_t[0], lanes([og[t] for t in range(4)]))
+        for t in range(4):
+            m_dev[me, t] = (m_own[t].astype(F32) + new[:, cols(t)]).astype(BF16)
+
+    def col_attention():
+        def normalise_m(t):
+            for s in (2 * t, 2 * t + 1):
+                ln_m[s] = layer_norm_t(m_all[s])
+
+        def project(t):
+            proj = round_bf16(mm(wci_p[1], pair(ln_m, 2 * t)))
+            put_pair(cq, 2 * t, subl([part(proj, 0, C), sigmoid(part(proj, 3, C))]))
+            put_pair(ckv, 2 * t, proj[C:3 * C])
+        pipeline([normalise_m, project], S // 2)
+        attend_columns(S, cmask)
 
         def update(t):
-            new = pair(m_all, 2 * t).astype(F32) + mm(wco_t[b], pair(og, 2 * t))
+            new = pair(m_all, 2 * t).astype(F32) + mm(wco_t[1], pair(og, 2 * t))
             put_pair(m_all, 2 * t, new.astype(BF16))
+        return update
+
+    def opm_halves(b, first):
+        def normalise_m(t):
+            for s in (2 * t, 2 * t + 1):
+                ln_m[s] = layer_norm_t(m_all[s])
 
         def halves(t):
             both = mm(w_opm_in[b], pair(ln_m, 2 * t))
             for s, x in ((2 * t, lo(both)), (2 * t + 1, hi(both))):
                 acs[rows_at(s, C), :] = x * msk[pl.ds(s, 1), :].astype(F32)
-        pipeline([update, normalise_m, halves], S // 2)
+        pipeline(first + [normalise_m, halves], S // 2)
 
     row_id = lax.broadcasted_iota(jnp.int32, (S, L2), 0)
     lane_id = lax.broadcasted_iota(jnp.int32, (S, L2), 1)
@@ -367,52 +489,52 @@
     def put_z(t, z2):
         put_pair(z_t, 2 * t, z2.astype(BF16))
 
-    def send_z(stage):
+    def send_z(stage, b, size):
         def turn(t, z2):
+            put_z(t, z2)
             z2 = round_bf16(z2)
             for r, x in ((0, lo(z2)), (1, hi(z2))):
                 z_snd[stage, 2 * t + r] = jnp.transpose(x).astype(BF16)
 
         def send(t):
             for o in range(1, N_DAP):
-                z_copy(stage, o, 2 * t, 2).start()
+                z_copy(stage, o, 2 * t, 2, 0, size).start()
             for n in (2 * t, 2 * t + 1):
                 z_rcv[stage, me * R + n] = z_snd[stage, n, my_rows, :]
-        return [turn, send]
-
-    def receive_z(stage, b):
-        for o in range(1, N_DAP):
-            z_copy(stage, o, 0, R).wait()
-
+        return [turn, normalise, bias_rows(bsc_tri, ln_t, b, 1), send]
+
+    def widen_z(stage, at, size):
         def widen(t):
             for r in range(4):
                 n = t * 4 + r
-                z_f[pl.ds(pl.multiple_of(n * (R + H), H), R), :] = z_rcv[stage, n].astype(F32)
+                z_f[pl.ds(pl.multiple_of(n * (R + H) + at, H), size), :] = z_rcv[stage, n, pl.ds(at, size), :].astype(F32)
         pipeline([widen], R)
 
-        def turn(t):
-            for n in (2 * t, 2 * t + 1):
-                z_t[n] = jnp.transpose(z_f[pl.ds(n, L, stride=R + H), :]).astype(BF16)
-        pipeline([turn, normalise, bias_rows(bsc_tri, ln_t, b, 1)], R // 2)
+    def wait_z(stage, at, size):
+        for o in range(1, N_DAP):
+            z_copy(stage, o, 0, R, at, size).wait()
+
+    def turn_z(t):
+        for n in (2 * t, 2 * t + 1):
+            z_t[n] = jnp.transpose(z_f[pl.ds(n, L, stride=R + H), :]).astype(BF16)
+
+    wait(g_in)
 
     def enter(t):
         for n in (2 * t, 2 * t + 1):
             z_t[n] = jnp.transpose(z_in[n].astype(F32)).astype(BF16)
     pipeline([enter, normalise, bias_rows(bsc_row, ln_t, 0, 0)], R // 2)
-    pack_bias(bsc_row, rb.at[0], 0, H)
-    g = gather(0, rb.at[0, :, my_rows, :])
+    row_attention_own()
+    col_attention_own()
+    g = gather(1, m_dev.at[me])
     start(g)
+    late_weights()
     wait(g)
-    for h in range(H):
-        bt_row[:, cols(h)] = jnp.transpose(rb[0, h].astype(F32)) * LOG2E
-
-    def store_m(s, value):
-        m_all[4 * me + s] = value
-    row_attention(0, lambda s: m_in[s], store_m)
-    g = gather(1, m_all.at[pl.ds(4 * me, 4)])
-    start(g)
-    wait(g)
-    col_attention(0)
+    for t in range(4):
+        whole = mm(lanes([m_dev[d, t] for d in range(4)]), join[...]).astype(BF16)
+        for k in range(4):
+            m_all[4 * t + k] = whole[:, cols(k)]
+    opm_halves(0, [])
 
     def add_first(n, update2):
         put_pair(z_t, n, (pair(z_t, n).astype(F32) + update2).astype(BF16))
@@ -420,28 +542,30 @@
     pack_bias(bsc_tri, tb.at[0], 0, 4)
     g = gather(2, tb.at[0, :, my_rows, :])
     start(g)
-    tri_project(w_ts_in.at[0])
+    pipeline(project_stages(w_ts_in.at[0]), R // 2)
     wait(g)
-    make_tri_bias(tb.at[0])
-    tri_attend(wtri_t.at[0, 0], send_z(0))
-
-    col_attention(1)
+    make_tri_bias(tb.at[0], False)
+    pipeline(attend_stages(wtri_t.at[0, 0], send_z(0, 0, R)), R // 2)
+    pack_bias(bsc_tri, tb.at[1], 4, 4)
+    g = gather(3, tb.at[1, :, my_rows, :])
+    start(g)
+
+    opm_halves(1, [col_attention()])
 
     def keep_update(n, update2):
         put_pair(u_opm, n, update2)
     opm(1, [keep_update])
 
-    receive_z(0, 0)
-    pack_bias(bsc_tri, tb.at[1], 4, 4)
-    g = gather(3, tb.at[1, :, my_rows, :])
-    start(g)
-    tri_project(w_te_in.at[0])
     wait(g)
-    make_tri_bias(tb.at[1])
-    tri_attend(wtri_t.at[1, 0], [put_z, normalise, bias_rows(bsc_row, ln_t, 1, 0)])
-
-    pack_bias(bsc_row, rb.at[1], 0, H)
-    g_row = gather(4, rb.at[1, :, my_rows, :])
+    make_tri_bias(tb.at[1], True)
+    wait_z(0, 0, R)
+    widen_z(0, 0, R)
+    pipeline(
+        [turn_z, normalise] + project_stages(w_te_in.at[0])
+        + attend_stages(wtri_t.at[1, 0], [put_z, normalise, bias_rows(bsc_row, ln_t, 1, 0)]), R // 2)
+
+    pack_bias(bsc_row, rb, 0, H)
+    g_row = gather(4, rb.at[:, my_rows, :])
     start(g_row)
 
     def add_second(t):
@@ -450,31 +574,54 @@
     pack_bias(bsc_tri, tb.at[2], 4, 4)
     g = gather(5, tb.at[2, :, my_rows, :])
     start(g)
-    tri_project(w_te_in.at[1])
+    pipeline(project_stages(w_te_in.at[1]), R // 2)
     wait(g)
-    make_tri_bias(tb.at[2])
-    tri_attend(wtri_t.at[1, 1], send_z(1))
-
-    wait(g_row)
-    for h in range(H):
-        bt_row[:, cols(h)] = rb[1, h].astype(F32) * LOG2E
-
-    def emit_m(s, value):
-        m_out[s] = value
-    row_attention(1, lambda s: m_all[4 * me + s], emit_m)
-
-    receive_z(1, 1)
+    make_tri_bias(tb.at[2], False)
+    pipeline(attend_stages(wtri_t.at[1, 1], send_z(1, 1, S)), R // 2)
+    for o in range(1, N_DAP):
+        z_copy(2, o, 0, R, S, S).start()
     pack_bias(bsc_tri, tb.at[3], 0, 4)
     g = gather(6, tb.at[3, :, my_rows, :])
     start(g)
-    tri_project(w_ts_in.at[1])
+
+    wait(g_row)
+    for h in range(H):
+        bt_row[:, cols(h)] = rb[h].astype(F32) * LOG2E
+
+    def emit_m(s, value):
+        m_own[s] = value
+    row_attention(1, lambda s: m_all[4 * me + s], emit_m)
+    m_done = pltpu.make_async_copy(m_own, m_out, in_sems.at[0])
+    m_done.start()
+
     wait(g)
-    make_tri_bias(tb.at[3])
+    make_tri_bias(tb.at[3], True)
 
     def emit_z(t, z2):
         for n, x in ((2 * t, lo(z2)), (2 * t + 1, hi(z2))):
-            z_out[n] = jnp.transpose(x).astype(BF16)
-    tri_attend(wtri_t.at[0, 1], [emit_z])
+            z_snd[0, n] = jnp.transpose(x).astype(BF16)
+
+    def put_out(n, count):
+        return pltpu.make_async_copy(z_snd.at[0, pl.ds(n, count)], z_out.at[pl.ds(n, count)], in_sems.at[1])
+
+    def leave(t):
+        put_out(2 * t, 2).start()
+
+    def second_half():
+        wait_z(2, S, S)
+        widen_z(1, S, S)
+    wait_z(1, 0, S)
+    widen_z(1, 0, S)
+    pipeline(
+        [turn_z, normalise] + project_stages(w_ts_in.at[1]) + attend_stages(wtri_t.at[0, 1], [emit_z, leave]),
+        R // 2, R // 4, second_half)
+    m_done.wait()
+    put_out(0, R).wait()
+
+
+def hand_out(m_new, z_new, m_out, z_out):
+    m_out[...] = m_new[...]
+    z_out[...] = z_new[...]
 
 
 def solution(mesh):
@@ -487,7 +634,7 @@
             return w.reshape(2, -1, w.shape[-1])
 
         w_bias = jnp.concatenate([jnp.swapaxes(w, 1, 2) for w in (w_row_bias, w_ts_bias, w_te_bias)], axis=1)
-        vmem = pl.BlockSpec(memory_space=pltpu.VMEM)
+        hbm = pl.BlockSpec(memory_space=pltpu.HBM)
 
         def wide(*shape):
             return pltpu.VMEM(shape, F32)
@@ -498,29 +645,45 @@
         scratch = dict(
             z_t=half(R, L, L), ln_t=half(R, L, L), p_q=half(R, L, L), p_kt=half(R, L, L), p_v=half(R, L, L),
             p_sg=wide(R, L, L), k_s=wide(L, L2), bsc_row=wide(R * H, L), bsc_tri=wide(R * H, L),
-            rb=half(2, H, L, L), tb=half(4, 4, L, L), bt_row=wide(L, H * L), bt_tri=wide(L, 4 * L),
-            m_all=half(S, C, L), ln_m=half(S, C, L), cp=wide(S, 4 * C, L), og=half(S, C, L),
-            cmask=wide(S, H, L), kcols=wide(4, L, L), mq=wide(4, C, L), mkt=half(4, L, C), mv=half(4, C, L),
+            rb=half(H, L, L), tb=half(4, 4, L, L), bt_row=wide(L, H * L), bt_tri=wide(L, 4 * L),
+            m_all=half(S, C, L), m_dev=half(4, 4, C, L), m_own=half(4, C, L), ln_m=half(S, C, L),
+            cq=wide(S, L, L), ckv=wide(S, L, L), og=half(S, C, L),
+            cmask=wide(S, H, L), omask=wide(S, H, L), kcols=wide(S, L, L),
+            mq=half(S, C, L2), mkt=half(S, L, C), mv=half(S, C, L),
+            pick=half(4 * L, L), spread=half(L, 8 * L), join=half(4 * L, 4 * L),
             acs=wide(S * C, L), r_all=half(R, S, L), x_loc=wide(L, R * S),
             o_scr=half(R, L, L), u_opm=wide(R, L, L), z_snd=half(2, R, L, L), z_rcv=half(2, L, R, L),
             z_f=wide(L * (R + H), L), nrm=wide(L, L), tmp=wide(R * R, L),
             wro_t=half(2, C, C), wci_p=half(2, 4 * C, C), wco_t=half(2, C, C), woo_t=half(2, L, R * R),
             wtri_t=half(2, 2, L, L), x_s=wide(4, L, L2), m_s=wide(4, 1, L2), w_s=half(4, L, L2), g_s=half(L, L2),
         )
-        sems = [pltpu.SemaphoreType.DMA((n, N_DAP - 1)) for n in (7, 7, 2, 2)]
-        m_new, z_new = pl.pallas_call(
-            body,
-            out_shape=(jax.ShapeDtypeStruct((4, C, L), BF16), jax.ShapeDtypeStruct((R, L, L), BF16)),
-            in_specs=[vmem] * 15,
-            out_specs=(vmem, vmem),
-            scratch_shapes=list(scratch.values()) + sems,
-            compiler_params=pltpu.CompilerParams(collective_id=0, has_side_effects=True, vmem_limit_bytes=60 * 2 ** 20),
-        )(
+        sems = [pltpu.SemaphoreType.DMA((n, N_DAP - 1)) for n in (7, 7, 3, 3)]
+        operands = (
             jnp.swapaxes(msa_act, 1, 2), pair_act, msa_mask, res_mask.reshape(1, L), w_bias,
             rows_first(w_row_in), flat_out(w_row_out), rows_first(w_col_in), flat_out(w_col_out),
             rows_first(w_opm_in), flat_out(w_opm_out),
             rows_first(w_ts_in), flat_out(w_ts_out), rows_first(w_te_in), flat_out(w_te_out),
         )
+        held = [pltpu.VMEM(x.shape, x.dtype) for x in operands[1:]] + [pltpu.SemaphoreType.DMA((N_IN,))]
+        m_new, z_new = pl.pallas_call(
+            body,
+            out_shape=(jax.ShapeDtypeStruct((4, C, L), BF16), jax.ShapeDtypeStruct((R, L, L), BF16)),
+            in_specs=[hbm] * N_IN,
+            out_specs=(hbm, hbm),
+            scratch_shapes=held + list(scratch.values()) + sems,
+            compiler_params=pltpu.CompilerParams(collective_id=0, has_side_effects=True, vmem_limit_bytes=60 * 2 ** 20),
+        )(*operands)
+        steps = 4
+
+        def blocks(array):
+            shape = (array.shape[0] // steps,) + array.shape[1:]
+            return pl.BlockSpec(shape, lambda k: (k, 0, 0))
+
+        specs = [blocks(m_new), blocks(z_new)]
+        m_new, z_new = pl.pallas_call(
+            hand_out, grid=(steps,), in_specs=specs, out_specs=specs,
+            out_shape=[jax.ShapeDtypeStruct(x.shape, x.dtype) for x in (m_new, z_new)],
+        )(m_new, z_new)
         return jnp.swapaxes(m_new, 1, 2), z_new
 
     in_specs = (P(('data', 'dap')), P(('data', 'dap')), P('data'), P('data')) + (P(),) * 13

time: 98.3 us -> 89.1 us (0.906)
  Pallas kernels: 92.3 us -> 86.9 us
  local copies, waits for them, and re-layouts: 4.47 us -> 0.69 us
    pallas_call x1, Pallas kernels: 92.3 us -> 83.5 us  [local_step(): pl.pallas_call(body, out_shape=(jax.ShapeDtypeStruct((4, C, L), BF16), ja...]
    unnamed x8 -> x6, local copies, waits for them, and re-layouts: 4.47 us -> 0.69 us
    pallas_call x0 -> x1, Pallas kernels: none -> 3.42 us  [local_step(): pl.pallas_call(hand_out, grid=(steps,), in_specs=specs, out_specs=specs,...]
where the time goes in v2:
time: 89.1 us; the launch traced here: 88.9 us
  Pallas kernels  86.9 us (98%)
    pallas_call x1, Pallas kernels, local_step(): pl.pallas_call(body, out_shape=(jax.ShapeDtypeStruct((4, C, L), BF16), ja...  83.5 us
    pallas_call x1, Pallas kernels, local_step(): pl.pallas_call(hand_out, grid=(steps,), in_specs=specs, out_specs=specs,...  3.42 us

profile of v2, /device:TPU:0, one launch (start us, length us, event | category | flops | bytes accessed | tf_op | source)
XLA Modules:
  0.0 88.9 jit_solution(16863064515989799161)
XLA Ops:
  0.6 0.0 copy-start.2
  0.6 0.0 copy-start
  0.7 0.0 copy-start.1
  0.7 0.7 copy-done.2
  1.3 0.0 copy-done
  1.3 0.0 copy-done.1
  1.3 0.6 pad_maximum_fusion.refs_3_
  2.0 83.5 %shard_map.176 = (bf16[4,64,128]{2,1,0:T(8,128)(2,1)}, bf16[32,128,128]{2,1,0:T(8,128)(2,1)}) custom-call(bf16[4,64,128]{2,1,0:T(8,128)(2,1)} %bitcast.31, bf16[32,128,128]{2,1,0:T(8,128)(2,1)} %refs_0_.1, s32[16,128]{1,0:T(8,128)} %refs_1_.1, s32[1,128]{1,0:T(1,128)} %bitcast.40, bf16[2,16,128]{2,1,0:T(8,128)(2,1)} %pad_maximum_fusion.refs_3_, ...), custom_call_target="tpu_custom_call" | custom-call | tf_op jit(solution)/shard_map/pallas_call | solution.py:668
  85.4 3.4 %shard_map.177 = (bf16[4,64,128]{2,1,0:T(8,128)(2,1)}, bf16[32,128,128]{2,1,0:T(8,128)(2,1)}) custom-call(bf16[4,64,128]{2,1,0:T(8,128)(2,1)} %get-tuple-element.6.m_new, bf16[32,128,128]{2,1,0:T(8,128)(2,1)} %get-tuple-element.7.z_new), custom_call_target="tpu_custom_call" | custom-call | tf_op jit(solution)/shard_map/pallas_call | solution.py:683
Async XLA Ops:
  0.6 0.7 copy-start.2
  0.6 0.7 copy-start
  0.7 0.7 copy-start.1

commit v3 on v2

--- a/solution.py
+++ b/solution.py
@@ -12,13 +12,14 @@
 LOG2E = 1.4426950408889634
 NEG = -1e9 * LOG2E
 N_DAP = 4
-N_IN = 15
+N_IN = 17
 L = 128
 R = 32
 S = 16
 C = 64
 H = 8
 L2 = 2 * L
+FIRST = 24
 MESH = pl.DeviceIdType.MESH
 
 
@@ -128,7 +129,7 @@
     m_hbm, given, held, in_sems, m_out, z_out,
     z_t, ln_t, p_q, p_kt, p_v, p_sg, k_s, bsc_row, bsc_tri, rb, tb, bt_row, bt_tri, m_all, m_dev, m_own, ln_m, cq, ckv, og,
     cmask, omask, kcols, mq, mkt, mv, pick, spread, join, acs, r_all, x_loc, o_scr, u_opm, z_snd, z_rcv, z_f, nrm, tmp, wro_t, wci_p, wco_t, woo_t, wtri_t,
-    x_s, m_s, w_s, g_s,
+    x_s, m_s, w_s, g_s, w_bias,
     g_send, g_recv, a_send, a_recv,
 ):
     me = lax.axis_index('dap')
@@ -138,8 +139,8 @@
     def peer(o):
         return (data, lax.rem(me + o, N_DAP))
 
-    z_in, msk, rmsk, w_bias, w_row_in, w_row_out, w_col_in, w_col_out, w_opm_in, w_opm_out = held[:10]
-    w_ts_in, w_ts_out, w_te_in, w_te_out = held[10:]
+    z_in, msk, rmsk, w_row_bias, w_ts_bias, w_te_bias = held[:6]
+    w_row_in, w_row_out, w_col_in, w_col_out, w_opm_in, w_opm_out, w_ts_in, w_ts_out, w_te_in, w_te_out = held[6:]
     own_m = m_all.at[pl.ds(4 * me, 4)]
     copy_m = pltpu.make_async_copy(m_hbm, own_m, in_sems.at[N_IN - 1])
     copy_m.start()
@@ -171,7 +172,7 @@
     def z_copy(stage, o, first, count, at=0, size=R):
         dest = lax.rem(me + o, N_DAP)
         return pltpu.make_async_remote_copy(
-            src_ref=z_snd.at[min(stage, 1), pl.ds(first, count), pl.ds(pl.multiple_of(dest * R + at, S), size), :],
+            src_ref=z_snd.at[min(stage, 1), pl.ds(first, count), pl.ds(pl.multiple_of(dest * R + at, H), size), :],
             dst_ref=z_rcv.at[min(stage, 1), pl.ds(me * R + first, count), pl.ds(at, size), :],
             send_sem=a_send.at[stage, o - 1], recv_sem=a_recv.at[stage, o - 1],
             device_id=(data, dest), device_id_type=MESH)
@@ -189,6 +190,10 @@
         return tmp[pl.ds(first, count, stride=stride), :]
 
     for b in range(2):
+        tmp[:H, :] = w_row_bias[b].astype(F32)
+        tmp[H:H + 4, :] = w_ts_bias[b].astype(F32)
+        tmp[H + 4:S, :] = w_te_bias[b].astype(F32)
+        w_bias[b] = tmp[:S, :].astype(BF16)
         wro_t[b] = mm_nt(e_c, w_row_out[b]).astype(BF16)
         tmp[:4 * C, :C] = w_col_in[b].astype(F32)
         wci_p[b] = subl([every(f * C + d, H, H) for f in range(4) for d in range(H)])[:, :C].astype(BF16)
@@ -577,12 +582,12 @@
     pipeline(project_stages(w_te_in.at[1]), R // 2)
     wait(g)
     make_tri_bias(tb.at[2], False)
-    pipeline(attend_stages(wtri_t.at[1, 1], send_z(1, 1, S)), R // 2)
-    for o in range(1, N_DAP):
-        z_copy(2, o, 0, R, S, S).start()
+    pipeline(attend_stages(wtri_t.at[1, 1], send_z(1, 1, FIRST)), R // 2)
     pack_bias(bsc_tri, tb.at[3], 0, 4)
     g = gather(6, tb.at[3, :, my_rows, :])
     start(g)
+    for o in range(1, N_DAP):
+        z_copy(2, o, 0, R, FIRST, R - FIRST).start()
 
     wait(g_row)
     for h in range(H):
@@ -607,21 +612,31 @@
     def leave(t):
         put_out(2 * t, 2).start()
 
-    def second_half():
-        wait_z(2, S, S)
-        widen_z(1, S, S)
-    wait_z(1, 0, S)
-    widen_z(1, 0, S)
+    def last_rows():
+        wait_z(2, FIRST, R - FIRST)
+        widen_z(1, FIRST, R - FIRST)
+    wait_z(1, 0, FIRST)
+    widen_z(1, 0, FIRST)
     pipeline(
         [turn_z, normalise] + project_stages(w_ts_in.at[1]) + attend_stages(wtri_t.at[0, 1], [emit_z, leave]),
-        R // 2, R // 4, second_half)
+        R // 2, FIRST // 2, last_rows)
     m_done.wait()
     put_out(0, R).wait()
 
 
-def hand_out(m_new, z_new, m_out, z_out):
-    m_out[...] = m_new[...]
-    z_out[...] = z_new[...]
+def hand_out(m_new, z_new, m_out, z_out, m_v, z_v, sems):
+    moves = [(m_new, m_v, m_out)]
+    for k in range(4):
+        moves.append([ref.at[pl.ds(k * H, H)] for ref in (z_new, z_v, z_out)])
+    into = [pltpu.make_async_copy(src, mid, sems.at[0, k]) for k, (src, mid, _) in enumerate(moves)]
+    out = [pltpu.make_async_copy(mid, dst, sems.at[1, k]) for k, (_, mid, dst) in enumerate(moves)]
+    for c in into:
+        c.start()
+    for c, d in zip(into, out):
+        c.wait()
+        d.start()
+    for d in out:
+        d.wait()
 
 
 def solution(mesh):
@@ -633,7 +648,7 @@
         def flat_out(w):
             return w.reshape(2, -1, w.shape[-1])
 
-        w_bias = jnp.concatenate([jnp.swapaxes(w, 1, 2) for w in (w_row_bias, w_ts_bias, w_te_bias)], axis=1)
+        w_bias = [jnp.swapaxes(w, 1, 2) for w in (w_row_bias, w_ts_bias, w_te_bias)]
         hbm = pl.BlockSpec(memory_space=pltpu.HBM)
 
         def wide(*shape):
@@ -655,11 +670,11 @@
             o_scr=half(R, L, L), u_opm=wide(R, L, L), z_snd=half(2, R, L, L), z_rcv=half(2, L, R, L),
             z_f=wide(L * (R + H), L), nrm=wide(L, L), tmp=wide(R * R, L),
             wro_t=half(2, C, C), wci_p=half(2, 4 * C, C), wco_t=half(2, C, C), woo_t=half(2, L, R * R),
-            wtri_t=half(2, 2, L, L), x_s=wide(4, L, L2), m_s=wide(4, 1, L2), w_s=half(4, L, L2), g_s=half(L, L2),
+            wtri_t=half(2, 2, L, L), x_s=wide(4, L, L2), m_s=wide(4, 1, L2), w_s=half(4, L, L2), g_s=half(L, L2), w_bias=half(2, S, L),
         )
         sems = [pltpu.SemaphoreType.DMA((n, N_DAP - 1)) for n in (7, 7, 3, 3)]
         operands = (
-            jnp.swapaxes(msa_act, 1, 2), pair_act, msa_mask, res_mask.reshape(1, L), w_bias,
+            jnp.swapaxes(msa_act, 1, 2), pair_act, msa_mask, res_mask.reshape(1, L), *w_bias,
             rows_first(w_row_in), flat_out(w_row_out), rows_first(w_col_in), flat_out(w_col_out),
             rows_first(w_opm_in), flat_out(w_opm_out),
             rows_first(w_ts_in), flat_out(w_ts_out), rows_first(w_te_in), flat_out(w_te_out),
@@ -673,16 +688,10 @@
             scratch_shapes=held + list(scratch.values()) + sems,
             compiler_params=pltpu.CompilerParams(collective_id=0, has_side_effects=True, vmem_limit_bytes=60 * 2 ** 20),
         )(*operands)
-        steps = 4
-
-        def blocks(array):
-            shape = (array.shape[0] // steps,) + array.shape[1:]
-            return pl.BlockSpec(shape, lambda k: (k, 0, 0))
-
-        specs = [blocks(m_new), blocks(z_new)]
         m_new, z_new = pl.pallas_call(
-            hand_out, grid=(steps,), in_specs=specs, out_specs=specs,
+            hand_out, in_specs=[hbm] * 2, out_specs=[hbm] * 2,
             out_shape=[jax.ShapeDtypeStruct(x.shape, x.dtype) for x in (m_new, z_new)],
+            scratch_shapes=[half(4, C, L), half(R, L, L), pltpu.SemaphoreType.DMA((2, 5))],
         )(m_new, z_new)
         return jnp.swapaxes(m_new, 1, 2), z_new
 

time: 89.1 us -> 83.6 us (0.938)
  Pallas kernels: 86.9 us -> 82.6 us
    pallas_call x1, Pallas kernels: 83.5 us -> 80.6 us  [local_step(): pl.pallas_call(body, out_shape=(jax.ShapeDtypeStruct((4, C, L), BF16), ja...]
    pallas_call x1, Pallas kernels: 3.42 us -> 2.04 us  [local_step(): pl.pallas_call(hand_out, in_specs=[hbm] * 2, out_specs=[hbm] * 2, out_sha...]
where the time goes in v3:
time: 83.6 us; the launch traced here: 83.4 us
  Pallas kernels  82.6 us (99%)
    pallas_call x1, Pallas kernels, local_step(): pl.pallas_call(body, out_shape=(jax.ShapeDtypeStruct((4, C, L), BF16), ja...  80.6 us
    pallas_call x1, Pallas kernels, local_step(): pl.pallas_call(hand_out, in_specs=[hbm] * 2, out_specs=[hbm] * 2, out_sha...  2.04 us

profile of v3, /device:TPU:0, one launch (start us, length us, event | category | flops | bytes accessed | tf_op | source)
XLA Modules:
  0.0 83.4 jit_solution(15099992648211950151)
XLA Ops:
  0.6 80.6 %shard_map.176 = (bf16[4,64,128]{2,1,0:T(8,128)(2,1)}, bf16[32,128,128]{2,1,0:T(8,128)(2,1)}) custom-call(bf16[4,64,128]{2,1,0:T(8,128)(2,1)} %bitcast.31, bf16[32,128,128]{2,1,0:T(8,128)(2,1)} %refs_0_.1, s32[16,128]{1,0:T(8,128)} %refs_1_.1, s32[1,128]{1,0:T(1,128)} %bitcast.40, bf16[2,8,128]{2,1,0:T(8,128)(2,1)} %bitcast.37, bf16[2,4,128]{2,1,0:T(4,128)(2,1)} %bitcast.38, ...), custom_call_target="tpu_custom_call" | custom-call | tf_op jit(solution)/shard_map/pallas_call | solution.py:683
  81.2 2.0 %shard_map.177 = (bf16[4,64,128]{2,1,0:T(8,128)(2,1)}, bf16[32,128,128]{2,1,0:T(8,128)(2,1)}) custom-call(bf16[4,64,128]{2,1,0:T(8,128)(2,1)} %get-tuple-element.6.m_new, bf16[32,128,128]{2,1,0:T(8,128)(2,1)} %get-tuple-element.7.z_new), custom_call_target="tpu_custom_call" | custom-call | tf_op jit(solution)/shard_map/pallas_call | solution.py:691

commit v4 on v3

--- a/solution.py
+++ b/solution.py
@@ -127,7 +127,7 @@
 
 def main(
     m_hbm, given, held, in_sems, m_out, z_out,
-    z_t, ln_t, p_q, p_kt, p_v, p_sg, k_s, bsc_row, bsc_tri, rb, tb, bt_row, bt_tri, m_all, m_dev, m_own, ln_m, cq, ckv, og,
+    z_t, ln_t, p_q, p_kt, p_v, p_sg, k_s, bsc_row, bsc_tri, rb, tb, bt_row, bt_tri, m_all, m_dev, c_dev, m_own, ln_m, cq, ckv, og,
     cmask, omask, kcols, mq, mkt, mv, pick, spread, join, acs, r_all, x_loc, o_scr, u_opm, z_snd, z_rcv, z_f, nrm, tmp, wro_t, wci_p, wco_t, woo_t, wtri_t,
     x_s, m_s, w_s, g_s, w_bias,
     g_send, g_recv, a_send, a_recv,
@@ -429,6 +429,15 @@
         new = mm(wco_t[0], lanes([og[t] for t in range(4)]))
         for t in range(4):
             m_dev[me, t] = (m_own[t].astype(F32) + new[:, cols(t)]).astype(BF16)
+        both = mm(w_opm_in[0], lanes([layer_norm_t(m_dev[me, t]) for t in range(4)]))
+        for t in range(4):
+            mask = omask[4 * t, :1]
+            for k in range(1, 4):
+                mask = jnp.where(block[:1] == k, omask[4 * t + k, :1], mask)
+            x = (both[:, cols(t)] * mask).astype(BF16)
+            c_dev[me, t] = part(x, 1, R)
+            for k in range(4):
+                acs[pl.ds((4 * t + k) * C, R), :] = mm(part(x, 0, R), spread[:, cols(2 * k)])
 
     def col_attention():
         def normalise_m(t):
@@ -473,7 +482,7 @@
         def outer(t):
             left = []
             for k in range(4):
-                row = x_loc[pl.ds(me * R + t * 4 + k, 1), :]
+                row = x_loc[pl.ds(b * me * R + t * 4 + k, 1), :]
                 for half in (cols(0, L2), cols(1, L2)):
                     left.append(jnp.where(diag, jnp.broadcast_to(row[:, half], (S, L2)), 0.0))
             left = subl(left).astype(BF16)
@@ -523,23 +532,23 @@
         for n in (2 * t, 2 * t + 1):
             z_t[n] = jnp.transpose(z_f[pl.ds(n, L, stride=R + H), :]).astype(BF16)
 
-    wait(g_in)
-
     def enter(t):
         for n in (2 * t, 2 * t + 1):
             z_t[n] = jnp.transpose(z_in[n].astype(F32)).astype(BF16)
     pipeline([enter, normalise, bias_rows(bsc_row, ln_t, 0, 0)], R // 2)
+    wait(g_in)
     row_attention_own()
     col_attention_own()
-    g = gather(1, m_dev.at[me])
+    g = gather(7, c_dev.at[me])
     start(g)
+    g_m = gather(1, m_dev.at[me])
+    start(g_m)
     late_weights()
     wait(g)
     for t in range(4):
-        whole = mm(lanes([m_dev[d, t] for d in range(4)]), join[...]).astype(BF16)
+        whole = mm(lanes([c_dev[d, t] for d in range(4)]), join[...])
         for k in range(4):
-            m_all[4 * t + k] = whole[:, cols(k)]
-    opm_halves(0, [])
+            acs[pl.ds((4 * t + k) * C + R, R), :] = whole[:, cols(k)]
 
     def add_first(n, update2):
         put_pair(z_t, n, (pair(z_t, n).astype(F32) + update2).astype(BF16))
@@ -555,6 +564,11 @@
     g = gather(3, tb.at[1, :, my_rows, :])
     start(g)
 
+    wait(g_m)
+    for t in range(4):
+        whole = mm(lanes([m_dev[d, t] for d in range(4)]), join[...]).astype(BF16)
+        for k in range(4):
+            m_all[4 * t + k] = whole[:, cols(k)]
     opm_halves(1, [col_attention()])
 
     def keep_update(n, update2):
@@ -661,7 +675,7 @@
             z_t=half(R, L, L), ln_t=half(R, L, L), p_q=half(R, L, L), p_kt=half(R, L, L), p_v=half(R, L, L),
             p_sg=wide(R, L, L), k_s=wide(L, L2), bsc_row=wide(R * H, L), bsc_tri=wide(R * H, L),
             rb=half(H, L, L), tb=half(4, 4, L, L), bt_row=wide(L, H * L), bt_tri=wide(L, 4 * L),
-            m_all=half(S, C, L), m_dev=half(4, 4, C, L), m_own=half(4, C, L), ln_m=half(S, C, L),
+            m_all=half(S, C, L), m_dev=half(4, 4, C, L), c_dev=half(4, 4, R, L), m_own=half(4, C, L), ln_m=half(S, C, L),
             cq=wide(S, L, L), ckv=wide(S, L, L), og=half(S, C, L),
             cmask=wide(S, H, L), omask=wide(S, H, L), kcols=wide(S, L, L),
             mq=half(S, C, L2), mkt=half(S, L, C), mv=half(S, C, L),
@@ -672,7 +686,7 @@
             wro_t=half(2, C, C), wci_p=half(2, 4 * C, C), wco_t=half(2, C, C), woo_t=half(2, L, R * R),
             wtri_t=half(2, 2, L, L), x_s=wide(4, L, L2), m_s=wide(4, 1, L2), w_s=half(4, L, L2), g_s=half(L, L2), w_bias=half(2, S, L),
         )
-        sems = [pltpu.SemaphoreType.DMA((n, N_DAP - 1)) for n in (7, 7, 3, 3)]
+        sems = [pltpu.SemaphoreType.DMA((n, N_DAP - 1)) for n in (8, 8, 3, 3)]
         operands = (
             jnp.swapaxes(msa_act, 1, 2), pair_act, msa_mask, res_mask.reshape(1, L), *w_bias,
             rows_first(w_row_in), flat_out(w_row_out), rows_first(w_col_in), flat_out(w_col_out),

time: 83.6 us -> 80.2 us (0.959)
  Pallas kernels: 82.6 us -> 79.2 us
    pallas_call x1, Pallas kernels: 80.6 us -> 77.2 us  [local_step(): pl.pallas_call(body, out_shape=(jax.ShapeDtypeStruct((4, C, L), BF16), ja...]
where the time goes in v4:
time: 80.2 us; the launch traced here: 80 us
  Pallas kernels  79.2 us (99%)
  between operations  0.81 us (1%)
    pallas_call x1, Pallas kernels, local_step(): pl.pallas_call(body, out_shape=(jax.ShapeDtypeStruct((4, C, L), BF16), ja...  77.2 us
    pallas_call x1, Pallas kernels, local_step(): pl.pallas_call(hand_out, in_specs=[hbm] * 2, out_specs=[hbm] * 2, out_sha...  2.04 us

profile of v4, /device:TPU:0, one launch (start us, length us, event | category | flops | bytes accessed | tf_op | source)
XLA Modules:
  0.0 80.0 jit_solution(6409412914206030864)
XLA Ops:
  0.6 77.2 %shard_map.176 = (bf16[4,64,128]{2,1,0:T(8,128)(2,1)}, bf16[32,128,128]{2,1,0:T(8,128)(2,1)}) custom-call(bf16[4,64,128]{2,1,0:T(8,128)(2,1)} %bitcast.31, bf16[32,128,128]{2,1,0:T(8,128)(2,1)} %refs_0_.1, s32[16,128]{1,0:T(8,128)} %refs_1_.1, s32[1,128]{1,0:T(1,128)} %bitcast.40, bf16[2,8,128]{2,1,0:T(8,128)(2,1)} %bitcast.37, bf16[2,4,128]{2,1,0:T(4,128)(2,1)} %bitcast.38, ...), custom_call_target="tpu_custom_call" | custom-call | tf_op jit(solution)/shard_map/pallas_call | solution.py:697
  77.8 2.0 %shard_map.177 = (bf16[4,64,128]{2,1,0:T(8,128)(2,1)}, bf16[32,128,128]{2,1,0:T(8,128)(2,1)}) custom-call(bf16[4,64,128]{2,1,0:T(8,128)(2,1)} %get-tuple-element.6.m_new, bf16[32,128,128]{2,1,0:T(8,128)(2,1)} %get-tuple-element.7.z_new), custom_call_target="tpu_custom_call" | custom-call | tf_op jit(solution)/shard_map/pallas_call | solution.py:705

commit v5 on v4

--- a/solution.py
+++ b/solution.py
@@ -95,8 +95,9 @@
     return x.astype(BF16).astype(F32)
 
 
-def pipeline(stages, trips, pause=None, resume=None):
+def pipeline(stages, trips, hooks=None):
     depth = len(stages)
+    hooks = hooks or {}
 
     def run(t, first, last):
         for k in reversed(range(first, last)):
@@ -106,12 +107,16 @@
         run(t, 0, depth)
         return carry
 
-    for t in range(depth - 1):
+    begin = depth - 1
+    for t in range(begin):
+        if t in hooks:
+            hooks[t]()
         run(t, 0, t + 1)
-    if pause is not None:
-        lax.fori_loop(depth - 1, pause, step, 0)
-        resume()
-    lax.fori_loop(depth - 1 if pause is None else pause, trips, step, 0)
+    for t in sorted(t for t in hooks if t >= begin):
+        lax.fori_loop(begin, t, step, 0)
+        hooks[t]()
+        begin = t
+    lax.fori_loop(begin, trips, step, 0)
     for t in range(depth - 1):
         run(trips + t, t + 1, depth)
 
@@ -389,6 +394,7 @@
         def project_out(t):
             m_own[t] = (m_own[t].astype(F32) + mm(wro_t[0], g_s[:C, :L])).astype(BF16)
 
+        wait(g_in)
         for t in range(4):
             queries(t)
         for t in range(S // 2):
@@ -536,7 +542,6 @@
         for n in (2 * t, 2 * t + 1):
             z_t[n] = jnp.transpose(z_in[n].astype(F32)).astype(BF16)
     pipeline([enter, normalise, bias_rows(bsc_row, ln_t, 0, 0)], R // 2)
-    wait(g_in)
     row_attention_own()
     col_attention_own()
     g = gather(7, c_dev.at[me])
@@ -584,8 +589,6 @@
         + attend_stages(wtri_t.at[1, 0], [put_z, normalise, bias_rows(bsc_row, ln_t, 1, 0)]), R // 2)
 
     pack_bias(bsc_row, rb, 0, H)
-    g_row = gather(4, rb.at[:, my_rows, :])
-    start(g_row)
 
     def add_second(t):
         put_z(t, pair(z_t, 2 * t).astype(F32) + pair(u_opm, 2 * t))
@@ -593,6 +596,8 @@
     pack_bias(bsc_tri, tb.at[2], 4, 4)
     g = gather(5, tb.at[2, :, my_rows, :])
     start(g)
+    g_row = gather(4, rb.at[:, my_rows, :])
+    start(g_row)
     pipeline(project_stages(w_te_in.at[1]), R // 2)
     wait(g)
     make_tri_bias(tb.at[2], False)
@@ -613,8 +618,9 @@
     m_done = pltpu.make_async_copy(m_own, m_out, in_sems.at[0])
     m_done.start()
 
-    wait(g)
-    make_tri_bias(tb.at[3], True)
+    def last_bias():
+        wait(g)
+        make_tri_bias(tb.at[3], True)
 
     def emit_z(t, z2):
         for n, x in ((2 * t, lo(z2)), (2 * t + 1, hi(z2))):
@@ -633,7 +639,7 @@
     widen_z(1, 0, FIRST)
     pipeline(
         [turn_z, normalise] + project_stages(w_ts_in.at[1]) + attend_stages(wtri_t.at[0, 1], [emit_z, leave]),
-        R // 2, FIRST // 2, last_rows)
+        R // 2, {4: last_bias, FIRST // 2: last_rows})
     m_done.wait()
     put_out(0, R).wait()
 

time: 80.2 us -> 79.1 us (0.986)
  Pallas kernels: 79.2 us -> 78.2 us
    pallas_call x1, Pallas kernels: 77.2 us -> 76.1 us  [local_step(): pl.pallas_call(body, out_shape=(jax.ShapeDtypeStruct((4, C, L), BF16), ja...]
where the time goes in v5:
time: 79.1 us; the launch traced here: 79 us
  Pallas kernels  78.2 us (99%)
  between operations  0.81 us (1%)
    pallas_call x1, Pallas kernels, local_step(): pl.pallas_call(body, out_shape=(jax.ShapeDtypeStruct((4, C, L), BF16), ja...  76.1 us
    pallas_call x1, Pallas kernels, local_step(): pl.pallas_call(hand_out, in_specs=[hbm] * 2, out_specs=[hbm] * 2, out_sha...  2.04 us

profile of v5, /device:TPU:0, one launch (start us, length us, event | category | flops | bytes accessed | tf_op | source)
XLA Modules:
  0.0 79.0 jit_solution(4594683696784756248)
XLA Ops:
  0.6 76.1 %shard_map.176 = (bf16[4,64,128]{2,1,0:T(8,128)(2,1)}, bf16[32,128,128]{2,1,0:T(8,128)(2,1)}) custom-call(bf16[4,64,128]{2,1,0:T(8,128)(2,1)} %bitcast.31, bf16[32,128,128]{2,1,0:T(8,128)(2,1)} %refs_0_.1, s32[16,128]{1,0:T(8,128)} %refs_1_.1, s32[1,128]{1,0:T(1,128)} %bitcast.40, bf16[2,8,128]{2,1,0:T(8,128)(2,1)} %bitcast.37, bf16[2,4,128]{2,1,0:T(4,128)(2,1)} %bitcast.38, ...), custom_call_target="tpu_custom_call" | custom-call | tf_op jit(solution)/shard_map/pallas_call | solution.py:703
  76.8 2.0 %shard_map.177 = (bf16[4,64,128]{2,1,0:T(8,128)(2,1)}, bf16[32,128,128]{2,1,0:T(8,128)(2,1)}) custom-call(bf16[4,64,128]{2,1,0:T(8,128)(2,1)} %get-tuple-element.6.m_new, bf16[32,128,128]{2,1,0:T(8,128)(2,1)} %get-tuple-element.7.z_new), custom_call_target="tpu_custom_call" | custom-call | tf_op jit(solution)/shard_map/pallas_call | solution.py:711

commit v6 on v5

--- a/solution.py
+++ b/solution.py
@@ -580,19 +580,21 @@
         put_pair(u_opm, n, update2)
     opm(1, [keep_update])
 
+    def add_second(t):
+        put_z(t, pair(z_t, 2 * t).astype(F32) + pair(u_opm, 2 * t))
+
     wait(g)
     make_tri_bias(tb.at[1], True)
     wait_z(0, 0, R)
     widen_z(0, 0, R)
     pipeline(
         [turn_z, normalise] + project_stages(w_te_in.at[0])
-        + attend_stages(wtri_t.at[1, 0], [put_z, normalise, bias_rows(bsc_row, ln_t, 1, 0)]), R // 2)
+        + attend_stages(wtri_t.at[1, 0], [
+            put_z, normalise, bias_rows(bsc_row, ln_t, 1, 0), add_second, normalise, bias_rows(bsc_tri, ln_t, 1, 1)]),
+        R // 2)
 
     pack_bias(bsc_row, rb, 0, H)
 
-    def add_second(t):
-        put_z(t, pair(z_t, 2 * t).astype(F32) + pair(u_opm, 2 * t))
-    pipeline([add_second, normalise, bias_rows(bsc_tri, ln_t, 1, 1)], R // 2)
     pack_bias(bsc_tri, tb.at[2], 4, 4)
     g = gather(5, tb.at[2, :, my_rows, :])
     start(g)

time: 79.1 us -> 77.3 us (0.977)
  Pallas kernels: 78.2 us -> 76.4 us
    pallas_call x1, Pallas kernels: 76.1 us -> 74.3 us  [local_step(): pl.pallas_call(body, out_shape=(jax.ShapeDtypeStruct((4, C, L), BF16), ja...]
where the time goes in v6:
time: 77.3 us; the launch traced here: 77.2 us
  Pallas kernels  76.4 us (99%)
  between operations  0.81 us (1%)
    pallas_call x1, Pallas kernels, local_step(): pl.pallas_call(body, out_shape=(jax.ShapeDtypeStruct((4, C, L), BF16), ja...  74.3 us
    pallas_call x1, Pallas kernels, local_step(): pl.pallas_call(hand_out, in_specs=[hbm] * 2, out_specs=[hbm] * 2, out_sha...  2.04 us

profile of v6, /device:TPU:0, one launch (start us, length us, event | category | flops | bytes accessed | tf_op | source)
XLA Modules:
  0.0 77.2 jit_solution(4981162601659301384)
XLA Ops:
  0.6 74.3 %shard_map.176 = (bf16[4,64,128]{2,1,0:T(8,128)(2,1)}, bf16[32,128,128]{2,1,0:T(8,128)(2,1)}) custom-call(bf16[4,64,128]{2,1,0:T(8,128)(2,1)} %bitcast.31, bf16[32,128,128]{2,1,0:T(8,128)(2,1)} %refs_0_.1, s32[16,128]{1,0:T(8,128)} %refs_1_.1, s32[1,128]{1,0:T(1,128)} %bitcast.40, bf16[2,8,128]{2,1,0:T(8,128)(2,1)} %bitcast.37, bf16[2,4,128]{2,1,0:T(4,128)(2,1)} %bitcast.38, ...), custom_call_target="tpu_custom_call" | custom-call | tf_op jit(solution)/shard_map/pallas_call | solution.py:705
  75.0 2.0 %shard_map.177 = (bf16[4,64,128]{2,1,0:T(8,128)(2,1)}, bf16[32,128,128]{2,1,0:T(8,128)(2,1)}) custom-call(bf16[4,64,128]{2,1,0:T(8,128)(2,1)} %get-tuple-element.6.m_new, bf16[32,128,128]{2,1,0:T(8,128)(2,1)} %get-tuple-element.7.z_new), custom_call_target="tpu_custom_call" | custom-call | tf_op jit(solution)/shard_map/pallas_call | solution.py:713

commit v7 on v6

--- a/solution.py
+++ b/solution.py
@@ -100,7 +100,7 @@
     hooks = hooks or {}
 
     def run(t, first, last):
-        for k in reversed(range(first, last)):
+        for k in sorted(range(first, last), key=lambda k: (not hasattr(stages[k], 'early'), -k)):
             stages[k](t - k)
 
     def step(t, carry):
@@ -521,7 +521,8 @@
                 z_copy(stage, o, 2 * t, 2, 0, size).start()
             for n in (2 * t, 2 * t + 1):
                 z_rcv[stage, me * R + n] = z_snd[stage, n, my_rows, :]
-        return [turn, normalise, bias_rows(bsc_tri, ln_t, b, 1), send]
+        send.early = True
+        return [turn, send, normalise, bias_rows(bsc_tri, ln_t, b, 1)]
 
     def widen_z(stage, at, size):
         def widen(t):

time: 77.3 us -> 76.9 us (level)
  no operation moved by 1% of the time
where the time goes in v7:
time: 76.9 us; the launch traced here: 76.8 us
  Pallas kernels  76 us (99%)
  between operations  0.81 us (1%)
    pallas_call x1, Pallas kernels, local_step(): pl.pallas_call(body, out_shape=(jax.ShapeDtypeStruct((4, C, L), BF16), ja...  74 us
    pallas_call x1, Pallas kernels, local_step(): pl.pallas_call(hand_out, in_specs=[hbm] * 2, out_specs=[hbm] * 2, out_sha...  2.04 us

profile of v7, /device:TPU:0, one launch (start us, length us, event | category | flops | bytes accessed | tf_op | source)
XLA Modules:
  0.0 76.8 jit_solution(2215878362878859362)
XLA Ops:
  0.6 74.0 %shard_map.176 = (bf16[4,64,128]{2,1,0:T(8,128)(2,1)}, bf16[32,128,128]{2,1,0:T(8,128)(2,1)}) custom-call(bf16[4,64,128]{2,1,0:T(8,128)(2,1)} %bitcast.31, bf16[32,128,128]{2,1,0:T(8,128)(2,1)} %refs_0_.1, s32[16,128]{1,0:T(8,128)} %refs_1_.1, s32[1,128]{1,0:T(1,128)} %bitcast.40, bf16[2,8,128]{2,1,0:T(8,128)(2,1)} %bitcast.37, bf16[2,4,128]{2,1,0:T(4,128)(2,1)} %bitcast.38, ...), custom_call_target="tpu_custom_call" | custom-call | tf_op jit(solution)/shard_map/pallas_call | solution.py:706
  74.6 2.0 %shard_map.177 = (bf16[4,64,128]{2,1,0:T(8,128)(2,1)}, bf16[32,128,128]{2,1,0:T(8,128)(2,1)}) custom-call(bf16[4,64,128]{2,1,0:T(8,128)(2,1)} %get-tuple-element.6.m_new, bf16[32,128,128]{2,1,0:T(8,128)(2,1)} %get-tuple-element.7.z_new), custom_call_target="tpu_custom_call" | custom-call | tf_op jit(solution)/shard_map/pallas_call | solution.py:714
